TPU v7x, 32 devices: a whole 2x2x4 slice. The times are simulated.
32 devices in a mesh: f: 8 (over z, y), h: 4 (over x, core).
Axes of the slice: x: 2, y: 2, z: 4, core: 2. Of those that a mesh axis runs over, the one named last changes fastest.
Arguments:
- x: bfloat16 [4096, 2048], P(None, 'h')
- g1: float32 [2048], P('h')
- g2: float32 [2048], P('h')
- w_gate: bfloat16 [2048, 8192], P('h', 'f')
- w_up: bfloat16 [2048, 8192], P('h', 'f')
- w_down: bfloat16 [8192, 2048], P('f', 'h')
- o: bfloat16 [4096, 2048], P(None, 'f')
- w_o: bfloat16 [2048, 2048], P('f', 'h')
- w_qkv: bfloat16 [2048, 3072], P('h', 'f')
Outputs:
- output 1: bfloat16 [4096, 2048], P(None, 'h')
- output 2: bfloat16 [4096, 3072], P(None, 'f')
All inputs are finite; a program needn't handle non-finite values.
Results may differ from a plain program's by a relative error of at most 0.00413217.
Values are sent between devices in bfloat16 or wider.
A program may use at most 1 GiB of HBM per device.

v0:
```python
import jax
import jax.numpy as jnp
from jax import lax
from jax.sharding import PartitionSpec as P

EPS = 1e-6


def _dot(a, b):
    return jnp.dot(a, b, preferred_element_type=jnp.float32)


def _norm(x, g, d):
    xf = x.astype(jnp.float32)
    ss = lax.psum(jnp.sum(xf * xf, axis=-1, keepdims=True), 'h')
    r = lax.rsqrt(ss / d + EPS)
    return (xf * r * g).astype(jnp.bfloat16)


def solution(mesh):
    h = mesh.shape['h']

    def body(x, g1, g2, w_gate, w_up, w_down, o, w_o, w_qkv):
        d = x.shape[1] * h
        n = _norm(x, g1, d)
        gt, up = lax.psum((_dot(n, w_gate), _dot(n, w_up)), 'h')
        a = (jax.nn.silu(gt) * up).astype(jnp.bfloat16)
        y = lax.psum(_dot(a, w_down) + _dot(o, w_o), 'f')
        x_next = (x.astype(jnp.float32) + y).astype(jnp.bfloat16)
        n1 = _norm(x_next, g2, d)
        qkv = lax.psum(_dot(n1, w_qkv), 'h').astype(jnp.bfloat16)
        return x_next, qkv

    in_specs = (P(None, 'h'), P('h'), P('h'), P('h', 'f'), P('h', 'f'), P('f', 'h'),
                P(None, 'f'), P('f', 'h'), P('h', 'f'))
    return jax.shard_map(body, mesh=mesh, in_specs=in_specs,
                         out_specs=(P(None, 'h'), P(None, 'f')), check_vma=False)
```

profile of v0, /device:TPU:0, one launch (start us, length us, event | category | flops | bytes accessed | tf_op | source)
XLA Modules:
  0.0 1039.3 jit_solution(5419482535264426877)
XLA Ops:
  7.2 0.0 copy-start
  7.2 0.0 all-reduce.7.cloned.1.call-start
  7.2 3.2 fusion.3
  10.5 12.7 %psum.42 = f32[4096,1]{0,1:T(1,128)S(1)} all-reduce(f32[4096,1]{0,1:T(1,128)S(1)} %bitcast.11), channel_id=1, replica_groups=mesh['f'=8,'h'=4] {'h'}, use_global_device_ids=true, to_apply=%region_1.0 | all-reduce | flops 4096 | bytes 32768 | tf_op jit(solution)/shard_map/psum | solution.py:15
  23.2 0.0 copy-start.1
  23.2 0.0 copy-start.3
  23.2 0.0 copy-start.6
  23.2 12.9 %fusion.12 = f32[4096,1024]{1,0:T(8,128)} fusion(bf16[512,1024]{1,0:T(8,128)(2,1)} %param.13, bf16[4096,512]{1,0:T(8,128)(2,1)} %param.9, f32[512]{0:T(512)} %param.10, f32[4096]{0:T(1024)S(1)} %bitcast.12), kind=kOutput, calls=%fused_computation.18 | convolution fusion | flops 4303355904 | bytes 22038528 | tf_op jit(solution)/shard_map/dot_general | solution.py:10
  36.2 0.0 copy-done.3
  36.2 8.1 fusion.14
  44.3 0.0 all-reduce.7.cloned.1.call-update
  44.3 0.2 all-reduce.5.cloned.1.call-start
  44.5 558.2 %all-reduce.7.cloned.1.call-done = (f32[4096,1024]{1,0:T(8,128)}, f32[4096,1024]{1,0:T(8,128)}) async-done(((f32[4096,1024]{1,0:T(8,128)}, f32[4096,1024]{1,0:T(8,128)}), (f32[4096,1024]{1,0:T(8,128)}, f32[4096,1024]{1,0:T(8,128)})) %all-reduce.7.cloned.1.call-update) | async-done | bytes 33554448 | tf_op jit(solution)/shard_map/psum | solution.py:26
  602.7 16.6 %fusion.7 = f32[4096,512]{1,0:T(8,128)} fusion(bf16[1024,512]{1,0:T(8,128)(2,1)S(1)} %copy-done.4, f32[4096,1024]{1,0:T(8,128)} %get-tuple-element.2, f32[4096,1024]{1,0:T(8,128)} %get-tuple-element.3), kind=kOutput, calls=%fused_computation.13 | convolution fusion | flops 4320133120 | bytes 42991616 | tf_op jit(solution)/shard_map/dot_general | solution.py:10
  619.3 0.0 copy-done.2
  619.3 7.8 convolution_add_fusion
  627.2 0.0 all-reduce.5.cloned.1.call-update
  627.2 0.0 copy-start.5
  627.2 0.0 copy-start.7
  627.2 268.7 %all-reduce.5.cloned.1.call-done = f32[4096,512]{1,0:T(8,128)} async-done(((f32[4096,512]{1,0:T(8,128)}), f32[4096,512]{1,0:T(8,128)}) %all-reduce.5.cloned.1.call-update) | async-done | bytes 8388624 | tf_op jit(solution)/shard_map/psum | solution.py:28
  895.9 7.8 fusion
  903.7 10.3 psum.46
  914.0 7.3 fusion.8
  921.3 111.2 %all-reduce.8 = bf16[4096,384]{1,0:T(8,128)(2,1)} all-reduce(f32[4096,384]{1,0:T(8,128)} %fusion.8), channel_id=1, replica_groups=mesh['f'=8,'h'=4] {'h'}, use_global_device_ids=true, to_apply=%region_7.8 | all-reduce | flops 1572864 | bytes 9437184 | tf_op jit(solution)/shard_map/psum | solution.py:31
  (10 shorter events, 0.1 us)
Async XLA Ops:
  7.2 612.2 %copy-start = (bf16[4096,256]{1,0:T(8,128)(2,1)S(1)}, bf16[4096,256]{1,0:T(8,128)(2,1)}, u32[]{:S(2)}) copy-start(bf16[4096,256]{1,0:T(8,128)(2,1)} %param.15) | copy-start | bytes 6291460
  7.2 595.5 %all-reduce.7.cloned.1.call-start = ((), (), s32[]{:S(2)}) async-start(), calls=%async_computation.1 | async-start | bytes 67108864 | tf_op jit(solution)/shard_map/psum | solution.py:26
  23.2 13.0 %copy-start.1 = (bf16[4096,512]{1,0:T(8,128)(2,1)S(1)}, bf16[4096,512]{1,0:T(8,128)(2,1)}, u32[]{:S(2)}) copy-start(bf16[4096,512]{1,0:T(8,128)(2,1)} %param.9) | copy-start | bytes 12582916
  23.2 13.0 %copy-start.3 = (bf16[512,1024]{1,0:T(8,128)(2,1)S(1)}, bf16[512,1024]{1,0:T(8,128)(2,1)}, u32[]{:S(2)}) copy-start(bf16[512,1024]{1,0:T(8,128)(2,1)} %param.12) | copy-start | bytes 3145732
  23.2 12.9 %copy-start.6 = (f32[512]{0:T(512)S(1)}, f32[512]{0:T(512)}, u32[]{:S(2)}) copy-start(f32[512]{0:T(512)} %param.10) | copy-start | bytes 6148
  44.3 558.4 %copy-start.4 = (bf16[1024,512]{1,0:T(8,128)(2,1)S(1)}, bf16[1024,512]{1,0:T(8,128)(2,1)}, u32[]{:S(2)}) copy-start(bf16[1024,512]{1,0:T(8,128)(2,1)} %param.14) | copy-start | bytes 3145732
  44.3 851.6 %all-reduce.5.cloned.1.call-start = ((), (), s32[]{:S(2)}) async-start(), calls=%async_computation | async-start | bytes 16777216 | tf_op jit(solution)/shard_map/psum | solution.py:28
  602.7 16.6 %copy-start.2 = (bf16[256,512]{1,0:T(8,128)(2,1)S(1)}, bf16[256,512]{1,0:T(8,128)(2,1)}, u32[]{:S(2)}) copy-start(bf16[256,512]{1,0:T(8,128)(2,1)} %param.16) | copy-start | bytes 786436
  627.2 286.8 %copy-start.5 = (bf16[512,384]{1,0:T(8,128)(2,1)S(1)}, bf16[512,384]{1,0:T(8,128)(2,1)}, u32[]{:S(2)}) copy-start(bf16[512,384]{1,0:T(8,128)(2,1)} %param.17) | copy-start | bytes 1179652
  627.2 286.8 %copy-start.7 = (f32[512]{0:T(512)S(1)}, f32[512]{0:T(512)}, u32[]{:S(2)}) copy-start(f32[512]{0:T(512)} %param.11) | copy-start | bytes 6148
Sparse Core Ops, SparseCore 0:
  44.4 558.2 all-reduce.6
  627.3 268.5 all-reduce.4
where the time goes:
time: 1040 us
  waiting for transfers between devices  827 us (80%)
  blocking collectives  134 us (13%)
  matrix products  52.7 us (5%)
  between operations  14.1 us (1%)
  other arithmetic  11.1 us (1%)
    psum x1, waiting for transfers between devices, body(): gt, up = lax.psum((_dot(n, w_gate), _dot(n, w_up)), 'h')  558 us
    psum x1, waiting for transfers between devices, body(): y = lax.psum(_dot(a, w_down) + _dot(o, w_o), 'f')  269 us
    psum x1, blocking collectives, body(): qkv = lax.psum(_dot(n1, w_qkv), 'h').astype(jnp.bfloat16)  111 us
    dot_general x5, matrix products, _dot(): return jnp.dot(a, b, preferred_element_type=jnp.float32)  52.7 us
    psum x2, blocking collectives, _norm(): ss = lax.psum(jnp.sum(xf * xf, axis=-1, keepdims=True), 'h')  23 us
  transfers between devices with their start and end apart: 2, of which 2 were waited for; matrix products, arithmetic and copies ran while one was open for 0% of the time, Pallas kernels for 0%

commit v1 on v0

v1 whole, which is shorter than its diff:
```python
import jax
import jax.numpy as jnp
from jax import lax
from jax.sharding import PartitionSpec as P

EPS = 1e-6


def _dot(a, b):
    return jnp.dot(a, b, preferred_element_type=jnp.float32)


def _norm(x, g):
    xf = x.astype(jnp.float32)
    r = lax.rsqrt(jnp.mean(xf * xf, axis=-1, keepdims=True) + EPS)
    return (xf * r * g).astype(jnp.bfloat16)


def solution(mesh):
    nh, nf = mesh.shape['h'], mesh.shape['f']

    def body(x, g1, g2, w_gate, w_up, w_down, o, w_o, w_qkv):
        h = lax.axis_index('h')
        f = lax.axis_index('f')
        t = x.shape[0] // nh
        ts = t // nf
        xt = lax.all_to_all(x, 'h', split_axis=0, concat_axis=1, tiled=True)
        g1, g2 = lax.all_gather((g1, g2), 'h', axis=0, tiled=True)
        wg, wu = (lax.all_gather(w, 'h', axis=0, tiled=True) for w in (w_gate, w_up))
        wd, wo = (lax.all_gather(w, 'h', axis=1, tiled=True) for w in (w_down, w_o))
        wq = lax.all_gather(w_qkv, 'h', axis=0, tiled=True)
        n = _norm(xt, g1)
        a = (jax.nn.silu(_dot(n, wg)) * _dot(n, wu)).astype(jnp.bfloat16)
        ot = lax.dynamic_slice_in_dim(o, h * t, t, axis=0)
        y = lax.psum_scatter(_dot(a, wd) + _dot(ot, wo), 'f', scatter_dimension=0, tiled=True)
        xs = lax.dynamic_slice_in_dim(xt, f * ts, ts, axis=0)
        xn = (xs.astype(jnp.float32) + y).astype(jnp.bfloat16)
        xg = lax.all_gather(xn, 'f', axis=0, tiled=True)
        n1 = _norm(xg, g2)
        q = _dot(n1, wq).astype(jnp.bfloat16)
        x_next = lax.all_to_all(xg, 'h', split_axis=1, concat_axis=0, tiled=True)
        qkv = lax.all_gather(q, 'h', axis=0, tiled=True)
        return x_next, qkv

    in_specs = (P(None, 'h'), P('h'), P('h'), P('h', 'f'), P('h', 'f'), P('f', 'h'),
                P(None, 'f'), P('f', 'h'), P('h', 'f'))
    return jax.shard_map(body, mesh=mesh, in_specs=in_specs,
                         out_specs=(P(None, 'h'), P(None, 'f')), check_vma=False)
```

time: 1040 us -> 504 us (0.48)
  waiting for transfers between devices: 827 us -> 272 us
  blocking collectives: 134 us -> 150 us
  local copies, waits for them, and re-layouts: 0.05 us -> 13.7 us
  matrix products: 52.7 us -> 40.1 us
    psum x2 -> x0, waiting for transfers between devices: 827 us -> none  [the longest x1 558 us: body(): gt, up = lax.psum((_dot(n, w_gate), _dot(n, w_up)), 'h')]
    reduce_scatter x0 -> x1, waiting for transfers between devices: none -> 147 us  [body(): lax.psum_scatter(_dot(a, wd) + _dot(ot, wo), 'f', scatter_dimension=0, ti...]
    psum x3 -> x0, blocking collectives: 134 us -> none  [the longest x1 111 us: body(): qkv = lax.psum(_dot(n1, w_qkv), 'h').astype(jnp.bfloat16)]
    all_gather x0 -> x7, waiting for transfers between devices: none -> 122 us  [the longest x1 66.7 us: body(): xg = lax.all_gather(xn, 'f', axis=0, tiled=True)]
    all_gather x0 -> x2, blocking collectives: none -> 81.8 us  [body(): g1, g2 = lax.all_gather((g1, g2), 'h', axis=0, tiled=True)]
    all_to_all x0 -> x1, blocking collectives: none -> 68.3 us  [body(): x_next = lax.all_to_all(xg, 'h', split_axis=1, concat_axis=0, tiled=True)]
    dot_general x5 -> x4, matrix products: 52.7 us -> 40.1 us  [_dot(): return jnp.dot(a, b, preferred_element_type=jnp.float32)]
  transfers between devices with their start and end apart: 2 -> 9, of which waited for: 2 -> 6; matrix products, arithmetic and copies ran while one was open for 0% -> 8% of each run, Pallas kernels for 0% -> 0%
where the time goes in v1:
time: 504 us
  waiting for transfers between devices  272 us (54%)
  blocking collectives  150 us (30%)
  matrix products  40.1 us (8%)
  between operations  14.2 us (3%)
  local copies, waits for them, and re-layouts  13.7 us (3%)
  other arithmetic  8.42 us (2%)
  starting transfers between devices  5.17 us (1%)
    reduce_scatter x1, waiting for transfers between devices, body(): lax.psum_scatter(_dot(a, wd) + _dot(ot, wo), 'f', scatter_dimension=0, ti...  147 us
    all_gather x2, blocking collectives, body(): g1, g2 = lax.all_gather((g1, g2), 'h', axis=0, tiled=True)  81.8 us
    all_to_all x1, blocking collectives, body(): x_next = lax.all_to_all(xg, 'h', split_axis=1, concat_axis=0, tiled=True)  68.3 us
    all_gather x1, waiting for transfers between devices, body(): xg = lax.all_gather(xn, 'f', axis=0, tiled=True)  66.7 us
    dot_general x4, matrix products, _dot(): return jnp.dot(a, b, preferred_element_type=jnp.float32)  40.1 us
    all_gather x2, waiting for transfers between devices, body(): wd, wo = (lax.all_gather(w, 'h', axis=1, tiled=True) for w in (w_down, w_o))  38.9 us
    all_gather x1, waiting for transfers between devices, body(): wq = lax.all_gather(w_qkv, 'h', axis=0, tiled=True)  16 us
  transfers between devices with their start and end apart: 9, of which 6 were waited for; matrix products, arithmetic and copies ran while one was open for 8% of the time, Pallas kernels for 0%

profile of v1, /device:TPU:0, one launch (start us, length us, event | category | flops | bytes accessed | tf_op | source)
XLA Modules:
  0.0 503.7 jit_solution(1538823577281722871)
XLA Ops:
  7.2 0.7 all-gather.10.cloned.1.call-update
  8.0 0.7 all-gather.12.cloned.1.call-update
  8.7 0.7 all-gather.14.cloned.1.call-update
  9.4 4.9 all-to-all-start
  14.9 76.4 %all-gather = f32[4,1,512]{2,1,0:T(1,128)S(1)} all-gather(f32[1,1,512]{2,1,0:T(1,128)S(1)} %bitcast.31), channel_id=1, replica_groups=mesh['f'=8,'h'=4] {'h'}, dimensions={0}, use_global_device_ids=true | all-gather | bytes 10240 | tf_op jit(solution)/shard_map/all_gather | solution.py:28
  91.4 4.8 copy.16
  96.2 3.1 multiply_reduce_fusion
  99.3 9.9 %fusion.10 = f32[1024,1024]{1,0:T(8,128)} fusion(bf16[2048,1024]{1,0:T(8,128)(2,1)} %all-gather.10.cloned.1.call-done, bf16[1024,2048]{1,0:T(8,128)(2,1)} %bitcast.24, f32[2048]{0:T(1024)S(1)} %bitcast.28, f32[1024]{0:T(1024)S(1)} %add_rsqrt_fusion.1), kind=kOutput, calls=%fused_computation.14 | convolution fusion | flops 4303355904 | bytes 12595200 | tf_op jit(solution)/shard_map/dot_general | solution.py:10
  109.6 36.9 %all-gather.14.cloned.1.call-done = bf16[1024,2048]{1,0:T(8,128)(2,1)} async-done(((bf16[1024,512]{1,0:T(8,128)(2,1)}), bf16[1024,2048]{1,0:T(8,128)(2,1)}) %all-gather.14.cloned.1.call-update) | async-done | bytes 4194320 | tf_op jit(solution)/shard_map/all_gather | solution.py:30
  146.5 16.0 %fusion.11 = f32[1024,2048]{1,0:T(8,128)} fusion(bf16[1024,2048]{1,0:T(8,128)(2,1)} %all-gather.14.cloned.1.call-done, f32[1024,1024]{1,0:T(8,128)} %fusion.10, bf16[2048,1024]{1,0:T(8,128)(2,1)} %all-gather.12.cloned.1.call-done, bf16[1024,2048]{1,0:T(8,128)(2,1)} %bitcast.25, f32[2048]{0:T(1024)S(1)} %bitcast.29, f32[1024]{0:T(1024)S(1)} %add_rsqrt_fusion.1), kind=kOutput, calls=%fused_computation.15 | convolution fusion | flops 8604614656 | bytes 25178112 | tf_op jit(solution)/shard_map/dot_general | solution.py:10
  162.6 1.9 all-gather.16.cloned.1.call-done
  164.5 8.2 %convolution_add_fusion = f32[1024,2048]{1,0:T(8,128)} fusion(f32[1024,2048]{1,0:T(8,128)} %fusion.11, bf16[256,2048]{1,0:T(8,128)(2,1)} %all-gather.16.cloned.1.call-done, bf16[4096,256]{1,0:T(8,128)(2,1)S(1)} %copy-done, s32[]{:T(128)S(6)} %select_n.7), kind=kOutput, calls=%fused_computation.7 | convolution fusion | flops 1075838976 | bytes 18350084 | tf_op jit(solution)/shard_map/dot_general | solution.py:10
  172.8 146.5 %reduce-scatter.2.cloned.1.call-done = f32[128,2048]{1,0:T(8,128)} async-done(((f32[1024,2048]{1,0:T(8,128)}), f32[128,2048]{1,0:T(8,128)}) %reduce-scatter.2.cloned.1.call-update) | async-done | bytes 1048592 | tf_op jit(solution)/shard_map/reduce_scatter | solution.py:35
  319.3 2.3 add_convert_fusion
  321.7 0.7 all-gather.20.cloned.1.call-update
  322.4 5.4 %all-gather.1 = f32[4,1,512]{2,1,0:T(1,128)S(1)} all-gather(f32[1,1,512]{2,1,0:T(1,128)S(1)} %bitcast.32), channel_id=1, replica_groups=mesh['f'=8,'h'=4] {'h'}, dimensions={0}, use_global_device_ids=true | all-gather | bytes 10240 | tf_op jit(solution)/shard_map/all_gather | solution.py:28
  327.8 66.7 %all-gather.18.cloned.1.call-done = bf16[1024,2048]{1,0:T(8,128)(2,1)} async-done(((bf16[128,2048]{1,0:T(8,128)(2,1)}), bf16[1024,2048]{1,0:T(8,128)(2,1)}) %all-gather.18.cloned.1.call-update) | async-done | bytes 4194320 | tf_op jit(solution)/shard_map/all_gather | solution.py:38
  394.5 3.1 fusion
  397.6 16.0 %all-gather.20.cloned.1.call-done = bf16[2048,384]{1,0:T(8,128)(2,1)} async-done(((bf16[512,384]{1,0:T(8,128)(2,1)}), bf16[2048,384]{1,0:T(8,128)(2,1)}) %all-gather.20.cloned.1.call-update) | async-done | bytes 1572880 | tf_op jit(solution)/shard_map/all_gather | solution.py:31
  413.6 5.9 %fusion.7 = bf16[1024,384]{1,0:T(8,128)(2,1)} fusion(bf16[2048,384]{1,0:T(8,128)(2,1)} %all-gather.20.cloned.1.call-done, bf16[1024,2048]{1,0:T(8,128)(2,1)} %all-gather.18.cloned.1.call-done, f32[2048]{0:T(1024)S(1)} %bitcast.30, f32[1024]{0:T(1024)S(1)} %add_rsqrt_fusion), kind=kOutput, calls=%fused_computation.13 | convolution fusion | flops 1619394560 | bytes 6565888 | tf_op jit(solution)/shard_map/dot_general | solution.py:10
  419.6 2.6 copy.18
  422.2 68.3 %all_to_all.38 = bf16[1024,4,512]{2,0,1:T(8,128)(2,1)} all-to-all(bf16[1024,4,512]{2,0,1:T(8,128)(2,1)S(1)} %bitcast.23), channel_id=1, replica_groups=mesh['f'=8,'h'=4] {'h'}, dimensions={1} | all-to-all | bytes 8388608 | tf_op jit(solution)/shard_map/all_to_all | solution.py:41
  490.5 4.6 copy.21
  495.1 1.7 copy.22
  (26 shorter events, 1.3 us)
Async XLA Ops:
  7.2 157.3 %copy-start = (bf16[4096,256]{1,0:T(8,128)(2,1)S(1)}, bf16[4096,256]{1,0:T(8,128)(2,1)}, u32[]{:S(2)}) copy-start(bf16[4096,256]{1,0:T(8,128)(2,1)} %param.15) | copy-start | bytes 6291460
  7.2 92.1 %all-gather.10.cloned.1.call-start = ((), (), s32[]{:S(2)}) async-start(), calls=%async_computation.3 | async-start | bytes 5242880 | tf_op jit(solution)/shard_map/all_gather | solution.py:29
  7.9 101.7 %all-gather.12.cloned.1.call-start = ((), (), s32[]{:S(2)}) async-start(), calls=%async_computation.4 | async-start | bytes 5242880 | tf_op jit(solution)/shard_map/all_gather | solution.py:29
  8.7 137.9 %all-gather.14.cloned.1.call-start = ((), (), s32[]{:S(2)}) async-start(), calls=%async_computation.5 | async-start | bytes 5242880 | tf_op jit(solution)/shard_map/all_gather | solution.py:30
  9.4 5.5 %copy-start.2 = (f32[512]{0:T(512)S(1)}, f32[512]{0:T(512)}, u32[]{:S(2)}) copy-start(f32[512]{0:T(512)} %param.10) | copy-start | bytes 6148
  9.4 81.9 %all-to-all-start = ((bf16[4,1024,512]{2,1,0:T(8,128)(2,1)}), bf16[4,1024,512]{2,1,0:T(8,128)(2,1)}, u32[]{:S(2)}, u32[]{:S(2)}) async-start(bf16[4,1024,512]{2,1,0:T(8,128)(2,1)} %bitcast.27), calls=%async_computation | async-start | bytes 8388608 | tf_op jit(solution)/shard_map/all_to_all | solution.py:27
  14.3 150.2 %all-gather.16.cloned.1.call-start = ((), (), s32[]{:S(2)}) async-start(), calls=%async_computation.6 | async-start | bytes 1310720 | tf_op jit(solution)/shard_map/all_gather | solution.py:30
  14.8 304.5 %reduce-scatter.2.cloned.1.call-start = ((), (), s32[]{:S(2)}) async-start(), calls=%async_computation.7 | async-start | bytes 9437184 | tf_op jit(solution)/shard_map/reduce_scatter | solution.py:35
  172.7 149.7 %copy-start.3 = (f32[512]{0:T(512)S(1)}, f32[512]{0:T(512)}, u32[]{:S(2)}) copy-start(f32[512]{0:T(512)} %param.11) | copy-start | bytes 6148
  172.7 221.8 %all-gather.18.cloned.1.call-start = ((), (), s32[]{:S(2)}) async-start(), calls=%async_computation.8 | async-start | bytes 4718592 | tf_op jit(solution)/shard_map/all_gather | solution.py:38
  321.6 92.0 %all-gather.20.cloned.1.call-start = ((), (), s32[]{:S(2)}) async-start(), calls=%async_computation.9 | async-start | bytes 1966080 | tf_op jit(solution)/shard_map/all_gather | solution.py:31
  322.4 168.1 %all-gather.22.cloned.1.call-start = ((), (), s32[]{:S(2)}) async-start(), calls=%async_computation.10 | async-start | bytes 3932160 | tf_op jit(solution)/shard_map/all_gather | solution.py:42
  490.5 4.6 copy-start.1
Sparse Core Ops, SparseCore 0:
  9.5 59.8 all-gather.9
  71.0 38.5 all-gather.11
  111.2 35.3 all-gather.13
  148.0 16.4 all-gather.15
  172.9 146.4 reduce-scatter.1
  321.9 72.5 all-gather.17
  396.1 17.5 all-gather.19
  419.7 45.4 all-gather.21

commit v2 on v0

v2 whole, which is shorter than its diff:
```python
import functools

import jax
import jax.numpy as jnp
from jax import lax
from jax.experimental import pallas as pl
from jax.experimental.pallas import tpu as pltpu
from jax.sharding import PartitionSpec as P

EPS = 1e-6
BF, F32 = jnp.bfloat16, jnp.float32
MESH = pl.DeviceIdType.MESH

NS = 4
NU = 16
NJ = 4
STAGES = 7


def _dot(a, b):
    return jnp.dot(a, b, preferred_element_type=F32)


def _kernel(d_model, x_ref, g1_ref, g2_ref, wg_ref, wu_ref, wd_ref, o_ref, wo_ref, wq_ref,
            outx_ref, outq_ref,
            xt, n, g1b, g2b, wg, wu, wd, wo, wq, ot, a, yb, yr, z0r, z1r, xg, nq, qb,
            loc, gs, gr, xs, xr, ws, wr, bs, br, ps, pr, qs, qr):
    f, h = lax.axis_index('f'), lax.axis_index('h')
    z, y = f // 2, f % 2
    z1, z0 = z // 2, z % 2
    xx, c = h // 2, h % 2
    pos = y * 4 + z0 * 2 + z1

    def hx(k):
        return 2 * ((xx + k // 2) % 2) + (c + k % 2) % 2

    def dev(ff, hh):
        return (ff, hh)

    ypeer = dev(z * 2 + (1 - y), h)
    z0peer = dev((z1 * 2 + (1 - z0)) * 2 + y, h)
    z1peer = dev(((1 - z1) * 2 + z0) * 2 + y, h)
    core, across = dev(f, hx(1)), dev(f, hx(2))

    def remote(src, dst, ssem, rsem, to):
        return pltpu.make_async_remote_copy(src_ref=src, dst_ref=dst, send_sem=ssem, recv_sem=rsem,
                                            device_id=to, device_id_type=MESH)

    bar = pltpu.get_barrier_semaphore()
    for k in range(1, 4):
        pl.semaphore_signal(bar, inc=1, device_id=dev(f, hx(k)), device_id_type=MESH)
    for i in range(1, 8):
        pl.semaphore_signal(bar, inc=1, device_id=dev((f + i) % 8, h), device_id_type=MESH)
    pl.semaphore_wait(bar, 10)

    jw = wg.shape[-1]

    def wcols(ref, j):
        return ref.at[:, pl.ds(j * jw, jw)]

    crows = pl.ds((f % 2) * 4, 4)

    def x_cross(k):
        return remote(x_ref.at[hx(k), f // 2, crows], xt.at[h, f // 2, crows],
                      xs.at[k], xr.at[k], dev(f, hx(k)))

    x_core = remote(x_ref.at[hx(1)], xt.at[h], xs.at[1], xr.at[1], core)
    x_cross(2).start()
    x_cross(3).start()
    gcopies = []
    for k in range(1, 4):
        gcopies.append(remote(g1_ref, g1b.at[h], gs.at[0, k], gr.at[0, k], dev(f, hx(k))))
        gcopies.append(remote(g2_ref, g2b.at[h], gs.at[1, k], gr.at[1, k], dev(f, hx(k))))
    for cp in gcopies:
        cp.start()
    x_core.start()

    def w_send(i, j, to, lane):
        src, dst = ((wg_ref, wg), (wu_ref, wu))[i]
        return remote(wcols(src, j), dst.at[j, h], ws.at[lane, i, j], wr.at[lane, i, j], to)

    def w_fwd(i, j):
        dst = (wg, wu)[i]
        return remote(dst.at[j, hx(2)], dst.at[j, hx(2)], ws.at[2, i, j], wr.at[2, i, j], core)

    big = ((wo_ref, wo), (wd_ref, wd), (wq_ref, wq))

    def b_send(i, to, lane):
        return remote(big[i][0], big[i][1].at[h], bs.at[lane, i], br.at[lane, i], to)

    def b_fwd(i):
        dst = big[i][1]
        return remote(dst.at[hx(2)], dst.at[hx(2)], bs.at[2, i], br.at[2, i], core)

    for j in range(NJ):
        for i in range(2):
            w_send(i, j, across, 0).start()
    for i in range(3):
        b_send(i, across, 0).start()

    lcopies = [pltpu.make_async_copy(x_ref.at[h], xt.at[h], loc.at[0]),
               pltpu.make_async_copy(g1_ref, g1b.at[h], loc.at[1]),
               pltpu.make_async_copy(g2_ref, g2b.at[h], loc.at[2]),
               pltpu.make_async_copy(o_ref.at[h], ot, loc.at[3])]
    for i in range(3):
        lcopies.append(pltpu.make_async_copy(big[i][0], big[i][1].at[h], loc.at[4 + i]))
    for j in range(NJ):
        lcopies.append(pltpu.make_async_copy(wcols(wg_ref, j), wg.at[j, h], loc.at[7 + 2 * j]))
        lcopies.append(pltpu.make_async_copy(wcols(wu_ref, j), wu.at[j, h], loc.at[8 + 2 * j]))
    for cp in lcopies:
        cp.start()
    for j in range(NJ):
        for i in range(2):
            w_send(i, j, core, 1).start()
    for i in range(3):
        b_send(i, core, 1).start()

    x_cross(2).wait_recv()
    x_cross(3).wait_recv()
    oth = pl.ds(2 * (1 - xx), 2)

    def x_bcast(i):
        view = xt.at[oth, f // 2, crows]
        return remote(view, view, xs.at[3 + i], xr.at[3 + i], dev((f + i) % 8, h))

    for i in range(1, 8):
        x_bcast(i).start()

    for i in range(2):
        w_send(i, 0, across, 0).wait_recv()
        w_fwd(i, 0).start()

    for cp in lcopies:
        cp.wait()
    for cp in gcopies:
        cp.wait_recv()
    x_core.wait_recv()
    for i in range(1, 8):
        x_bcast(i).wait_recv()

    dh = xt.shape[-1]
    urows = 8 * xt.shape[3]

    @pl.loop(0, NS)
    def _(s):
        blocks = [xt[b, s].reshape(urows, dh).astype(F32) for b in range(4)]
        ss = functools.reduce(jnp.add, [jnp.sum(v * v, axis=-1, keepdims=True) for v in blocks])
        r = lax.rsqrt(ss / d_model + EPS)
        for b in range(4):
            n[s, :, b * dh:(b + 1) * dh] = (blocks[b] * r * g1b[b]).astype(BF)

    for j in range(NJ):
        for i in range(2):
            if j > 0:
                w_send(i, j, across, 0).wait_recv()
                w_fwd(i, j).start()
        for i in range(2):
            w_send(i, j, core, 1).wait_recv()
            w_fwd(i, j).wait_recv()
        wgj = wg.at[j]
        wuj = wu.at[j]

        @pl.loop(0, NS)
        def _(s):
            ns = n[s]
            gt = _dot(ns, wgj[...].reshape(4 * dh, jw))
            up = _dot(ns, wuj[...].reshape(4 * dh, jw))
            a[s, :, j * jw:(j + 1) * jw] = (jax.nn.silu(gt) * up).astype(BF)

    for i in range(3):
        b_send(i, core, 1).wait_recv()

    def st_y(u):
        return remote(yb.at[u, pl.ds((1 - y) * 4, 4)], yr.at[u], ps.at[0, u], pr.at[0, u], ypeer)

    def st_z0(u):
        return remote(yb.at[u, pl.ds(y * 4 + (1 - z0) * 2, 2)], z0r.at[u], ps.at[1, u], pr.at[1, u], z0peer)

    def st_z1(u):
        return remote(yb.at[u, y * 4 + z0 * 2 + (1 - z1)], z1r.at[u], ps.at[2, u], pr.at[2, u], z1peer)

    def ag_z1(u):
        v = xg.at[u, y, pl.ds(z0 * 2 + z1, 1)]
        return remote(v, v, ps.at[3, u], pr.at[3, u], z1peer)

    def ag_y(u):
        v = xg.at[u, y, pl.ds(z0 * 2, 2)]
        return remote(v, v, ps.at[4, u], pr.at[4, u], ypeer)

    def ag_z0(u):
        v = xg.at[u, :, pl.ds(z0 * 2, 2)]
        return remote(v, v, ps.at[5, u], pr.at[5, u], z0peer)

    def out_x(u, to_h):
        return remote(xg.at[u], outx_ref.at[h * NS + u // 4], ps.at[6, u], pr.at[6, u], dev(f, to_h))

    def out_x_local(u):
        return pltpu.make_async_copy(xg.at[u], outx_ref.at[h * NS + u // 4], ps.at[6, u])

    def out_q(s, k):
        return remote(qb.at[s], outq_ref.at[h * NS + s], qs.at[k, s], qr.at[k, s], dev(f, hx(k)))

    def out_q_local(s):
        return pltpu.make_async_copy(qb.at[s], outq_ref.at[h * NS + s], qs.at[0, s])

    def at(t, lag, fn):
        u = t - lag

        @pl.when((u >= 0) & (u < NU))
        def _():
            fn(u)

    def p_compute(u):
        s, b = u // 4, hx(u % 4)

        @pl.when(u == 2)
        def _():
            for i in range(3):
                b_send(i, across, 0).wait_recv()
                b_fwd(i).start()

        @pl.when(u == 3)
        def _():
            for i in range(3):
                b_fwd(i).wait_recv()

        v = _dot(a[s], wd[b]) + _dot(ot[s], wo[b])
        yb[u] = v.reshape(yb.shape[1:])
        st_y(u).start()

    def p_y(u):
        st_y(u).wait_recv()
        rows = pl.ds(y * 4, 4)
        yb[u, rows] = yb[u, rows] + yr[u]
        st_z0(u).start()

    def p_z0(u):
        st_z0(u).wait_recv()
        rows = pl.ds(y * 4 + z0 * 2, 2)
        yb[u, rows] = yb[u, rows] + z0r[u]
        st_z1(u).start()

    def p_z1(u):
        st_z1(u).wait_recv()
        s, b = u // 4, hx(u % 4)
        v = yb[u, pos] + z1r[u]
        xg[u, y, z0 * 2 + z1] = (xt[b, s, pos].astype(F32) + v).astype(BF)
        ag_z1(u).start()

    def p_ag_z1(u):
        ag_z1(u).wait_recv()
        ag_y(u).start()

    def p_ag_y(u):
        ag_y(u).wait_recv()
        ag_z0(u).start()

    def p_out(u):
        ag_z0(u).wait_recv()

        @pl.when(u % 4 == 0)
        def _():
            out_x_local(u).start()

        @pl.when(u % 4 != 0)
        def _():
            out_x(u, hx(u % 4)).start()

        @pl.when(u % 4 == 3)
        def _():
            s = u // 4
            blocks = [xg[4 * s + k].reshape(urows, dh).astype(F32) for k in range(4)]
            ss = functools.reduce(jnp.add, [jnp.sum(v * v, axis=-1, keepdims=True) for v in blocks])
            r = lax.rsqrt(ss / d_model + EPS)
            for k in range(4):
                nq[k] = (blocks[k] * r * g2b[hx(k)]).astype(BF)
            acc = functools.reduce(jnp.add, [_dot(nq[k], wq[hx(k)]) for k in range(4)])
            qb[s] = acc.astype(BF)
            for k in (2, 3, 1):
                out_q(s, k).start()
            out_q_local(s).start()

    @pl.loop(0, NU + 8)
    def _(t):
        at(t, 0, p_compute)
        at(t, 2, p_y)
        at(t, 3, p_z0)
        at(t, 4, p_z1)
        at(t, 5, p_ag_z1)
        at(t, 6, p_ag_y)
        at(t, 7, p_out)

    for cp in gcopies:
        cp.wait_send()
    x_core.wait_send()
    x_cross(2).wait_send()
    x_cross(3).wait_send()
    for i in range(1, 8):
        x_bcast(i).wait_send()
    for j in range(NJ):
        for i in range(2):
            w_send(i, j, across, 0).wait_send()
            w_send(i, j, core, 1).wait_send()
            w_fwd(i, j).wait_send()
    for i in range(3):
        b_send(i, across, 0).wait_send()
        b_send(i, core, 1).wait_send()
        b_fwd(i).wait_send()

    @pl.loop(0, NU)
    def _(u):
        st_y(u).wait_send()
        st_z0(u).wait_send()
        st_z1(u).wait_send()
        ag_z1(u).wait_send()
        ag_y(u).wait_send()
        ag_z0(u).wait_send()

        @pl.when(u % 4 == 0)
        def _():
            out_x_local(u).wait()

        @pl.when(u % 4 != 0)
        def _():
            k = u % 4
            rows = outx_ref.at[hx(k) * NS + u // 4]
            remote(xg.at[u], rows, ps.at[6, u], pr.at[6, u], dev(f, hx(k))).wait()

    @pl.loop(0, NS)
    def _(s):
        out_q_local(s).wait()
        for k in range(1, 4):
            remote(qb.at[s], outq_ref.at[hx(k) * NS + s], qs.at[k, s], qr.at[k, s], dev(f, hx(k))).wait()


def _block(x, g1, g2, w_gate, w_up, w_down, o, w_o, w_qkv):
    tokens, dh = x.shape
    tq = tokens // 4
    ur = tq // NS
    ch = ur // 8
    ff, ko, nqk = w_gate.shape[1], o.shape[1], w_qkv.shape[1]
    jw = ff // NJ
    any_ = pl.BlockSpec(memory_space=pl.ANY)
    dma = pltpu.SemaphoreType.DMA
    scratch = [
        pltpu.VMEM((4, NS, 8, ch, dh), BF),
        pltpu.VMEM((NS, ur, 4 * dh), BF),
        pltpu.VMEM((4, 1, dh), F32),
        pltpu.VMEM((4, 1, dh), F32),
        pltpu.VMEM((NJ, 4, dh, jw), BF),
        pltpu.VMEM((NJ, 4, dh, jw), BF),
        pltpu.VMEM((4, ff, dh), BF),
        pltpu.VMEM((4, ko, dh), BF),
        pltpu.VMEM((4, dh, nqk), BF),
        pltpu.VMEM((NS, ur, ko), BF),
        pltpu.VMEM((NS, ur, ff), BF),
        pltpu.VMEM((NU, 8, ch, dh), F32),
        pltpu.VMEM((NU, 4, ch, dh), F32),
        pltpu.VMEM((NU, 2, ch, dh), F32),
        pltpu.VMEM((NU, ch, dh), F32),
        pltpu.VMEM((NU, 2, 4, ch, dh), BF),
        pltpu.VMEM((4, ur, dh), BF),
        pltpu.VMEM((NS, ur, nqk), BF),
        dma((15,)),
        dma((2, 4)), dma((2, 4)),
        dma((11,)), dma((11,)),
        dma((3, 2, NJ)), dma((3, 2, NJ)),
        dma((3, 3)), dma((3, 3)),
        dma((STAGES, NU)), dma((STAGES, NU)),
        dma((4, NS)), dma((4, NS)),
    ]
    outx, outq = pl.pallas_call(
        functools.partial(_kernel, 4 * dh),
        name="block",
        out_shape=(jax.ShapeDtypeStruct((4 * NS, 2, 4, ch, dh), BF),
                   jax.ShapeDtypeStruct((4 * NS, ur, nqk), BF)),
        in_specs=[any_] * 9,
        out_specs=(any_, any_),
        scratch_shapes=scratch,
        compiler_params=pltpu.CompilerParams(collective_id=0, has_side_effects=True,
                                             vmem_limit_bytes=67043328),
    )(x.reshape(4, NS, 8, ch, dh), g1.reshape(1, dh), g2.reshape(1, dh), w_gate, w_up, w_down,
      o.reshape(4, NS, ur, ko), w_o, w_qkv)
    return outx.reshape(tokens, dh), outq.reshape(tokens, nqk)


def solution(mesh):
    in_specs = (P(None, 'h'), P('h'), P('h'), P('h', 'f'), P('h', 'f'), P('f', 'h'),
                P(None, 'f'), P('f', 'h'), P('h', 'f'))
    return jax.shard_map(_block, mesh=mesh, in_specs=in_specs,
                         out_specs=(P(None, 'h'), P(None, 'f')), check_vma=False)
```

time: 1040 us -> 255 us (0.25)
  waiting for transfers between devices: 827 us -> 0 us
  Pallas kernels: 0 us -> 248 us
  blocking collectives: 134 us -> 0 us
  matrix products: 52.7 us -> 0 us
  between operations: 14.1 us -> 0.65 us
  other arithmetic: 11.1 us -> 0 us
    psum x2 -> x0, waiting for transfers between devices: 827 us -> none  [the longest x1 558 us: body(): gt, up = lax.psum((_dot(n, w_gate), _dot(n, w_up)), 'h')]
    pallas_call x0 -> x1, Pallas kernels: none -> 248 us  [_block(): pl.pallas_call(functools.partial(_kernel, 4 * dh), name='block', out_shap...]
    psum x3 -> x0, blocking collectives: 134 us -> none  [the longest x1 111 us: body(): qkv = lax.psum(_dot(n1, w_qkv), 'h').astype(jnp.bfloat16)]
    dot_general x5 -> x0, matrix products: 52.7 us -> none  [_dot(): return jnp.dot(a, b, preferred_element_type=jnp.float32)]
    reduce_sum x2 -> x0, other arithmetic: 11 us -> none  [_norm(): ss = lax.psum(jnp.sum(xf * xf, axis=-1, keepdims=True), 'h')]
  transfers between devices with their start and end apart: 2 -> 0, of which waited for: 2 -> 0; matrix products, arithmetic and copies ran while one was open for 0% -> 0% of each run, Pallas kernels for 0% -> 0%
where the time goes in v2:
time: 255 us
  Pallas kernels  248 us (97%)
  local copies, waits for them, and re-layouts  6.3 us (2%)
    pallas_call x1, Pallas kernels, _block(): pl.pallas_call(functools.partial(_kernel, 4 * dh), name='block', out_shap...  248 us
    unnamed x4, local copies, waits for them, and re-layouts  6.3 us

profile of v2, /device:TPU:0, one launch (start us, length us, event | category | flops | bytes accessed | tf_op | source)
XLA Modules:
  0.0 254.5 jit_solution(12230651434592973720)
XLA Ops:
  0.6 247.6 %block.1 = (bf16[16,2,4,32,512]{4,3,2,1,0:T(8,128)(2,1)}, bf16[16,256,384]{2,1,0:T(8,128)(2,1)}) custom-call(bf16[4,4,8,32,512]{4,3,2,1,0:T(8,128)(2,1)} %bitcast.6, f32[1,512]{1,0:T(1,128)} %bitcast.10, f32[1,512]{1,0:T(1,128)} %bitcast.11, bf16[512,1024]{1,0:T(8,128)(2,1)} %wg_ref.1, bf16[512,1024]{1,0:T(8,128)(2,1)} %wu_ref.1, bf16[1024,512]{1,0:T(8,128)(2,1)} %wd_ref.1, ...), custom_call_target="tpu_custom_call" | custom-call | tf_op jit(solution)/shard_map/block/pallas_call | solution.py:372
  248.2 0.0 copy-start
  248.2 4.6 %copy.13 = bf16[4096,512]{1,0:T(8,128)(2,1)} copy(bf16[4096,512]{1,0:T(8,128)(2,1)} %bitcast.7) | data formatting | bytes 8388608
  252.8 0.0 copy-done
  252.8 1.7 copy.14
Async XLA Ops:
  248.2 4.6 %copy-start = (bf16[16,256,384]{2,1,0:T(8,128)(2,1)S(1)}, bf16[16,256,384]{2,1,0:T(8,128)(2,1)}, u32[]{:S(2)}) copy-start(bf16[16,256,384]{2,1,0:T(8,128)(2,1)} %get-tuple-element.5) | copy-start | bytes 9437188

commit v3 on v2

--- a/solution.py
+++ b/solution.py
@@ -14,7 +14,7 @@
 NS = 4
 NU = 16
 NJ = 4
-STAGES = 7
+STAGES = 5
 
 
 def _dot(a, b):
@@ -23,13 +23,11 @@
 
 def _kernel(d_model, x_ref, g1_ref, g2_ref, wg_ref, wu_ref, wd_ref, o_ref, wo_ref, wq_ref,
             outx_ref, outq_ref,
-            xt, n, g1b, g2b, wg, wu, wd, wo, wq, ot, a, yb, yr, z0r, z1r, xg, nq, qb,
-            loc, gs, gr, xs, xr, ws, wr, bs, br, ps, pr, qs, qr):
+            xt, n, g1b, g2b, wg, wu, wd, wo, wq, ot, a, yb, yr, upr, dnr, xg, nq, qb,
+            loc, gs, gr, xs, xr, ws, wr, bs, br, ps, pr, zs, zr, qs, qr):
     f, h = lax.axis_index('f'), lax.axis_index('h')
     z, y = f // 2, f % 2
-    z1, z0 = z // 2, z % 2
     xx, c = h // 2, h % 2
-    pos = y * 4 + z0 * 2 + z1
 
     def hx(k):
         return 2 * ((xx + k // 2) % 2) + (c + k % 2) % 2
@@ -38,8 +36,7 @@
         return (ff, hh)
 
     ypeer = dev(z * 2 + (1 - y), h)
-    z0peer = dev((z1 * 2 + (1 - z0)) * 2 + y, h)
-    z1peer = dev(((1 - z1) * 2 + z0) * 2 + y, h)
+    above, below = dev((f + 2) % 8, h), dev((f + 6) % 8, h)
     core, across = dev(f, hx(1)), dev(f, hx(2))
 
     def remote(src, dst, ssem, rsem, to):
@@ -119,12 +116,21 @@
     x_cross(3).wait_recv()
     oth = pl.ds(2 * (1 - xx), 2)
 
-    def x_bcast(i):
+    def x_z(i):
         view = xt.at[oth, f // 2, crows]
-        return remote(view, view, xs.at[3 + i], xr.at[3 + i], dev((f + i) % 8, h))
-
-    for i in range(1, 8):
-        x_bcast(i).start()
+        return remote(view, view, xs.at[3 + i], xr.at[3 + i], dev((f + 2 * i) % 8, h))
+
+    def x_y(i):
+        src = (f + 8 - 2 * i) % 8
+        view = xt.at[oth, src // 2, pl.ds((src % 2) * 4, 4)]
+        return remote(view, view, xs.at[7 + i], xr.at[7 + i], ypeer)
+
+    for i in (1, 3, 2):
+        x_z(i).start()
+    x_y(0).start()
+    for i in (1, 3, 2):
+        x_z(i).wait_recv()
+        x_y(i).start()
 
     for i in range(2):
         w_send(i, 0, across, 0).wait_recv()
@@ -135,8 +141,8 @@
     for cp in gcopies:
         cp.wait_recv()
     x_core.wait_recv()
-    for i in range(1, 8):
-        x_bcast(i).wait_recv()
+    for i in range(4):
+        x_y(i).wait_recv()
 
     dh = xt.shape[-1]
     urows = 8 * xt.shape[3]
@@ -173,29 +179,27 @@
     def st_y(u):
         return remote(yb.at[u, pl.ds((1 - y) * 4, 4)], yr.at[u], ps.at[0, u], pr.at[0, u], ypeer)
 
-    def st_z0(u):
-        return remote(yb.at[u, pl.ds(y * 4 + (1 - z0) * 2, 2)], z0r.at[u], ps.at[1, u], pr.at[1, u], z0peer)
-
-    def st_z1(u):
-        return remote(yb.at[u, y * 4 + z0 * 2 + (1 - z1)], z1r.at[u], ps.at[2, u], pr.at[2, u], z1peer)
-
-    def ag_z1(u):
-        v = xg.at[u, y, pl.ds(z0 * 2 + z1, 1)]
-        return remote(v, v, ps.at[3, u], pr.at[3, u], z1peer)
+    def st_up(u, zz):
+        return remote(yb.at[u, pl.ds(y * 4 + zz + 1, 3 - zz)], upr.at[u, pl.ds(zz, 3 - zz)],
+                      ps.at[1, u], pr.at[1, u], above)
+
+    def st_dn(u, zz):
+        return remote(yb.at[u, pl.ds(y * 4, zz)], dnr.at[u, pl.ds(0, zz)],
+                      ps.at[2, u], pr.at[2, u], below)
 
     def ag_y(u):
-        v = xg.at[u, y, pl.ds(z0 * 2, 2)]
-        return remote(v, v, ps.at[4, u], pr.at[4, u], ypeer)
-
-    def ag_z0(u):
-        v = xg.at[u, :, pl.ds(z0 * 2, 2)]
-        return remote(v, v, ps.at[5, u], pr.at[5, u], z0peer)
+        v = xg.at[u, y, pl.ds(z, 1)]
+        return remote(v, v, ps.at[3, u], pr.at[3, u], ypeer)
+
+    def ag_z(u, src, way):
+        v = xg.at[u, :, pl.ds(src, 1)]
+        return remote(v, v, zs.at[way, u, src], zr.at[u, src], (above, below)[way])
 
     def out_x(u, to_h):
-        return remote(xg.at[u], outx_ref.at[h * NS + u // 4], ps.at[6, u], pr.at[6, u], dev(f, to_h))
+        return remote(xg.at[u], outx_ref.at[h * NS + u // 4], ps.at[4, u], pr.at[4, u], dev(f, to_h))
 
     def out_x_local(u):
-        return pltpu.make_async_copy(xg.at[u], outx_ref.at[h * NS + u // 4], ps.at[6, u])
+        return pltpu.make_async_copy(xg.at[u], outx_ref.at[h * NS + u // 4], ps.at[4, u])
 
     def out_q(s, k):
         return remote(qb.at[s], outq_ref.at[h * NS + s], qs.at[k, s], qr.at[k, s], dev(f, hx(k)))
@@ -227,36 +231,97 @@
         v = _dot(a[s], wd[b]) + _dot(ot[s], wo[b])
         yb[u] = v.reshape(yb.shape[1:])
         st_y(u).start()
+
+    def send_up(u, zz):
+        @pl.when(z == zz)
+        def _():
+            if zz > 0:
+                st_up(u, zz - 1).wait_recv()
+                for q in range(zz + 1, 4):
+                    yb[u, y * 4 + q] = yb[u, y * 4 + q] + upr[u, q - 1]
+            st_up(u, zz).start()
+
+    def send_dn(u, zz):
+        @pl.when(z == zz)
+        def _():
+            if zz < 3:
+                st_dn(u, zz + 1).wait_recv()
+                for q in range(zz):
+                    yb[u, y * 4 + q] = yb[u, y * 4 + q] + dnr[u, q]
+            st_dn(u, zz).start()
 
     def p_y(u):
         st_y(u).wait_recv()
         rows = pl.ds(y * 4, 4)
         yb[u, rows] = yb[u, rows] + yr[u]
-        st_z0(u).start()
-
-    def p_z0(u):
-        st_z0(u).wait_recv()
-        rows = pl.ds(y * 4 + z0 * 2, 2)
-        yb[u, rows] = yb[u, rows] + z0r[u]
-        st_z1(u).start()
-
-    def p_z1(u):
-        st_z1(u).wait_recv()
+        send_up(u, 0)
+        send_dn(u, 3)
+
+    def p_h2(u):
+        send_up(u, 1)
+        send_dn(u, 2)
+
+    def p_h3(u):
+        send_up(u, 2)
+        send_dn(u, 1)
+
+    def p_fin(u):
         s, b = u // 4, hx(u % 4)
-        v = yb[u, pos] + z1r[u]
-        xg[u, y, z0 * 2 + z1] = (xt[b, s, pos].astype(F32) + v).astype(BF)
-        ag_z1(u).start()
-
-    def p_ag_z1(u):
-        ag_z1(u).wait_recv()
+        own = xt[b, s, y * 4 + z].astype(F32)
+
+        @pl.when(z == 0)
+        def _():
+            st_dn(u, 1).wait_recv()
+            xg[u, y, 0] = (own + (yb[u, y * 4] + dnr[u, 0])).astype(BF)
+
+        @pl.when(z == 3)
+        def _():
+            st_up(u, 2).wait_recv()
+            xg[u, y, 3] = (own + (yb[u, y * 4 + 3] + upr[u, 2])).astype(BF)
+
+        @pl.when((z == 1) | (z == 2))
+        def _():
+            v = yb[u, y * 4 + z] + upr[u, z - 1] + dnr[u, z]
+            xg[u, y, z] = (own + v).astype(BF)
+
         ag_y(u).start()
 
-    def p_ag_y(u):
+    def p_g1(u):
         ag_y(u).wait_recv()
-        ag_z0(u).start()
+
+        @pl.when(z < 3)
+        def _():
+            ag_z(u, z, 0).start()
+
+        @pl.when(z > 0)
+        def _():
+            ag_z(u, z, 1).start()
+
+    def p_fwd(u, d):
+        @pl.when(z >= d)
+        def _():
+            ag_z(u, z - d, 0).wait_recv()
+
+        @pl.when((z >= d) & (z < 3))
+        def _():
+            ag_z(u, z - d, 0).start()
+
+        @pl.when(z + d <= 3)
+        def _():
+            ag_z(u, z + d, 1).wait_recv()
+
+        @pl.when((z + d <= 3) & (z > 0))
+        def _():
+            ag_z(u, z + d, 1).start()
+
+    def p_g2(u):
+        p_fwd(u, 1)
+
+    def p_g3(u):
+        p_fwd(u, 2)
 
     def p_out(u):
-        ag_z0(u).wait_recv()
+        p_fwd(u, 3)
 
         @pl.when(u % 4 == 0)
         def _():
@@ -276,27 +341,39 @@
                 nq[k] = (blocks[k] * r * g2b[hx(k)]).astype(BF)
             acc = functools.reduce(jnp.add, [_dot(nq[k], wq[hx(k)]) for k in range(4)])
             qb[s] = acc.astype(BF)
-            for k in (2, 3, 1):
+            for k in (2, 1):
                 out_q(s, k).start()
             out_q_local(s).start()
 
-    @pl.loop(0, NU + 8)
+    def out_q_from(s, k):
+        rows = outq_ref.at[hx(k) * NS + s]
+        return remote(qb.at[s], rows, qs.at[k, s], qr.at[k, s], dev(f, hx(k)))
+
+    def q_fwd(s):
+        rows = outq_ref.at[hx(2) * NS + s]
+        return remote(rows, rows, qs.at[3, s], qr.at[3, s], core)
+
+    def p_q(u):
+        @pl.when(u % 4 == 3)
+        def _():
+            out_q_from(u // 4, 2).wait_recv()
+            q_fwd(u // 4).start()
+
+    @pl.loop(0, NU + 10)
     def _(t):
-        at(t, 0, p_compute)
-        at(t, 2, p_y)
-        at(t, 3, p_z0)
-        at(t, 4, p_z1)
-        at(t, 5, p_ag_z1)
-        at(t, 6, p_ag_y)
-        at(t, 7, p_out)
+        for lag, fn in ((0, p_compute), (2, p_y), (3, p_h2), (4, p_h3), (5, p_fin), (6, p_g1),
+                        (7, p_g2), (8, p_g3), (9, p_out), (10, p_q)):
+            at(t, lag, fn)
 
     for cp in gcopies:
         cp.wait_send()
     x_core.wait_send()
     x_cross(2).wait_send()
     x_cross(3).wait_send()
-    for i in range(1, 8):
-        x_bcast(i).wait_send()
+    for i in range(4):
+        x_y(i).wait_send()
+    for i in range(1, 4):
+        x_z(i).wait_send()
     for j in range(NJ):
         for i in range(2):
             w_send(i, j, across, 0).wait_send()
@@ -310,11 +387,24 @@
     @pl.loop(0, NU)
     def _(u):
         st_y(u).wait_send()
-        st_z0(u).wait_send()
-        st_z1(u).wait_send()
-        ag_z1(u).wait_send()
+        for zz in range(3):
+            @pl.when(z == zz)
+            def _():
+                st_up(u, zz).wait_send()
+
+            @pl.when(z == zz + 1)
+            def _():
+                st_dn(u, zz + 1).wait_send()
+
         ag_y(u).wait_send()
-        ag_z0(u).wait_send()
+        for d in range(3):
+            @pl.when((z >= d) & (z < 3))
+            def _():
+                ag_z(u, z - d, 0).wait_send()
+
+            @pl.when((z + d <= 3) & (z > 0))
+            def _():
+                ag_z(u, z + d, 1).wait_send()
 
         @pl.when(u % 4 == 0)
         def _():
@@ -324,13 +414,15 @@
         def _():
             k = u % 4
             rows = outx_ref.at[hx(k) * NS + u // 4]
-            remote(xg.at[u], rows, ps.at[6, u], pr.at[6, u], dev(f, hx(k))).wait()
+            remote(xg.at[u], rows, ps.at[4, u], pr.at[4, u], dev(f, hx(k))).wait()
 
     @pl.loop(0, NS)
     def _(s):
         out_q_local(s).wait()
-        for k in range(1, 4):
-            remote(qb.at[s], outq_ref.at[hx(k) * NS + s], qs.at[k, s], qr.at[k, s], dev(f, hx(k))).wait()
+        out_q_from(s, 1).wait()
+        out_q_from(s, 2).wait_send()
+        q_fwd(s).wait_send()
+        out_q_from(s, 3).wait_recv()
 
 
 def _block(x, g1, g2, w_gate, w_up, w_down, o, w_o, w_qkv):
@@ -356,8 +448,8 @@
         pltpu.VMEM((NS, ur, ff), BF),
         pltpu.VMEM((NU, 8, ch, dh), F32),
         pltpu.VMEM((NU, 4, ch, dh), F32),
-        pltpu.VMEM((NU, 2, ch, dh), F32),
-        pltpu.VMEM((NU, ch, dh), F32),
+        pltpu.VMEM((NU, 3, ch, dh), F32),
+        pltpu.VMEM((NU, 3, ch, dh), F32),
         pltpu.VMEM((NU, 2, 4, ch, dh), BF),
         pltpu.VMEM((4, ur, dh), BF),
         pltpu.VMEM((NS, ur, nqk), BF),
@@ -367,6 +459,7 @@
         dma((3, 2, NJ)), dma((3, 2, NJ)),
         dma((3, 3)), dma((3, 3)),
         dma((STAGES, NU)), dma((STAGES, NU)),
+        dma((2, NU, 4)), dma((NU, 4)),
         dma((4, NS)), dma((4, NS)),
     ]
     outx, outq = pl.pallas_call(

time: 255 us -> 244 us (0.957)
  Pallas kernels: 248 us -> 237 us
    pallas_call x1, Pallas kernels: 248 us -> 237 us  [_block(): pl.pallas_call(functools.partial(_kernel, 4 * dh), name='block', out_shap...]
where the time goes in v3:
time: 244 us
  Pallas kernels  237 us (97%)
  local copies, waits for them, and re-layouts  6.3 us (3%)
    pallas_call x1, Pallas kernels, _block(): pl.pallas_call(functools.partial(_kernel, 4 * dh), name='block', out_shap...  237 us
    unnamed x4, local copies, waits for them, and re-layouts  6.3 us

profile of v3, /device:TPU:0, one launch (start us, length us, event | category | flops | bytes accessed | tf_op | source)
XLA Modules:
  0.0 243.7 jit_solution(14786139250854162467)
XLA Ops:
  0.6 236.7 %block.1 = (bf16[16,2,4,32,512]{4,3,2,1,0:T(8,128)(2,1)}, bf16[16,256,384]{2,1,0:T(8,128)(2,1)}) custom-call(bf16[4,4,8,32,512]{4,3,2,1,0:T(8,128)(2,1)} %bitcast.6, f32[1,512]{1,0:T(1,128)} %bitcast.10, f32[1,512]{1,0:T(1,128)} %bitcast.11, bf16[512,1024]{1,0:T(8,128)(2,1)} %wg_ref.1, bf16[512,1024]{1,0:T(8,128)(2,1)} %wu_ref.1, bf16[1024,512]{1,0:T(8,128)(2,1)} %wd_ref.1, ...), custom_call_target="tpu_custom_call" | custom-call | tf_op jit(solution)/shard_map/block/pallas_call | solution.py:465
  237.4 0.0 copy-start
  237.4 4.6 %copy.13 = bf16[4096,512]{1,0:T(8,128)(2,1)} copy(bf16[4096,512]{1,0:T(8,128)(2,1)} %bitcast.7) | data formatting | bytes 8388608
  242.0 0.0 copy-done
  242.0 1.7 copy.14
Async XLA Ops:
  237.4 4.6 %copy-start = (bf16[16,256,384]{2,1,0:T(8,128)(2,1)S(1)}, bf16[16,256,384]{2,1,0:T(8,128)(2,1)}, u32[]{:S(2)}) copy-start(bf16[16,256,384]{2,1,0:T(8,128)(2,1)} %get-tuple-element.5) | copy-start | bytes 9437188

commit v4 on v3

--- a/solution.py
+++ b/solution.py
@@ -11,8 +11,9 @@
 BF, F32 = jnp.bfloat16, jnp.float32
 MESH = pl.DeviceIdType.MESH
 
-NS = 4
-NU = 16
+NS = 8
+NU = 32
+NE = 6
 NJ = 4
 STAGES = 5
 
@@ -55,10 +56,9 @@
     def wcols(ref, j):
         return ref.at[:, pl.ds(j * jw, jw)]
 
-    crows = pl.ds((f % 2) * 4, 4)
 
     def x_cross(k):
-        return remote(x_ref.at[hx(k), f // 2, crows], xt.at[h, f // 2, crows],
+        return remote(x_ref.at[hx(k), f], xt.at[h, f],
                       xs.at[k], xr.at[k], dev(f, hx(k)))
 
     x_core = remote(x_ref.at[hx(1)], xt.at[h], xs.at[1], xr.at[1], core)
@@ -117,12 +117,12 @@
     oth = pl.ds(2 * (1 - xx), 2)
 
     def x_z(i):
-        view = xt.at[oth, f // 2, crows]
+        view = xt.at[oth, f]
         return remote(view, view, xs.at[3 + i], xr.at[3 + i], dev((f + 2 * i) % 8, h))
 
     def x_y(i):
         src = (f + 8 - 2 * i) % 8
-        view = xt.at[oth, src // 2, pl.ds((src % 2) * 4, 4)]
+        view = xt.at[oth, src]
         return remote(view, view, xs.at[7 + i], xr.at[7 + i], ypeer)
 
     for i in (1, 3, 2):
@@ -166,12 +166,13 @@
         wgj = wg.at[j]
         wuj = wu.at[j]
 
-        @pl.loop(0, NS)
-        def _(s):
-            ns = n[s]
+        @pl.loop(0, NS // 2)
+        def _(i):
+            ns = n[pl.ds(2 * i, 2)].reshape(2 * urows, 4 * dh)
             gt = _dot(ns, wgj[...].reshape(4 * dh, jw))
             up = _dot(ns, wuj[...].reshape(4 * dh, jw))
-            a[s, :, j * jw:(j + 1) * jw] = (jax.nn.silu(gt) * up).astype(BF)
+            v = (jax.nn.silu(gt) * up).astype(BF)
+            a[pl.ds(2 * i, 2), :, j * jw:(j + 1) * jw] = v.reshape(2, urows, jw)
 
     for i in range(3):
         b_send(i, core, 1).wait_recv()
@@ -208,24 +209,27 @@
         return pltpu.make_async_copy(qb.at[s], outq_ref.at[h * NS + s], qs.at[0, s])
 
     def at(t, lag, fn):
-        u = t - lag
-
-        @pl.when((u >= 0) & (u < NU))
-        def _():
-            fn(u)
+        i = t - lag
+
+        @pl.when((i >= 0) & (i < NU))
+        def _():
+            late = i // (4 * NE)
+            s = (1 - late) * ((i % (2 * NE)) // 2) + late * (i // 4)
+            k = (1 - late) * (2 * (i // (2 * NE)) + i % 2) + late * ((i + 2) % 4)
+            fn(4 * s + k)
 
     def p_compute(u):
         s, b = u // 4, hx(u % 4)
 
         @pl.when(u == 2)
         def _():
-            for i in range(3):
+            for i in range(2):
                 b_send(i, across, 0).wait_recv()
                 b_fwd(i).start()
 
         @pl.when(u == 3)
         def _():
-            for i in range(3):
+            for i in range(2):
                 b_fwd(i).wait_recv()
 
         v = _dot(a[s], wd[b]) + _dot(ot[s], wo[b])
@@ -287,6 +291,11 @@
         ag_y(u).start()
 
     def p_g1(u):
+        @pl.when(u == 3)
+        def _():
+            b_send(2, across, 0).wait_recv()
+            b_fwd(2).start()
+
         ag_y(u).wait_recv()
 
         @pl.when(z < 3)
@@ -320,9 +329,16 @@
     def p_g3(u):
         p_fwd(u, 2)
 
+    def done(u):
+        return ((u % 4 == 3) & (u < 4 * NE)) | ((u % 4 == 1) & (u >= 4 * NE))
+
     def p_out(u):
         p_fwd(u, 3)
 
+        @pl.when(u == 3)
+        def _():
+            b_fwd(2).wait_recv()
+
         @pl.when(u % 4 == 0)
         def _():
             out_x_local(u).start()
@@ -331,7 +347,7 @@
         def _():
             out_x(u, hx(u % 4)).start()
 
-        @pl.when(u % 4 == 3)
+        @pl.when(done(u))
         def _():
             s = u // 4
             blocks = [xg[4 * s + k].reshape(urows, dh).astype(F32) for k in range(4)]
@@ -354,7 +370,7 @@
         return remote(rows, rows, qs.at[3, s], qr.at[3, s], core)
 
     def p_q(u):
-        @pl.when(u % 4 == 3)
+        @pl.when(done(u))
         def _():
             out_q_from(u // 4, 2).wait_recv()
             q_fwd(u // 4).start()
@@ -465,13 +481,13 @@
     outx, outq = pl.pallas_call(
         functools.partial(_kernel, 4 * dh),
         name="block",
-        out_shape=(jax.ShapeDtypeStruct((4 * NS, 2, 4, ch, dh), BF),
-                   jax.ShapeDtypeStruct((4 * NS, ur, nqk), BF)),
+        out_shape=(pltpu.VMEM((4 * NS, 2, 4, ch, dh), BF),
+                   pltpu.VMEM((4 * NS, ur, nqk), BF)),
         in_specs=[any_] * 9,
         out_specs=(any_, any_),
         scratch_shapes=scratch,
         compiler_params=pltpu.CompilerParams(collective_id=0, has_side_effects=True,
-                                             vmem_limit_bytes=67043328),
+                                             vmem_limit_bytes=56 * 2**20),
     )(x.reshape(4, NS, 8, ch, dh), g1.reshape(1, dh), g2.reshape(1, dh), w_gate, w_up, w_down,
       o.reshape(4, NS, ur, ko), w_o, w_qkv)
     return outx.reshape(tokens, dh), outq.reshape(tokens, nqk)

time: 244 us -> 221 us (0.906)
  Pallas kernels: 237 us -> 216 us
  local copies, waits for them, and re-layouts: 6.3 us -> 3.68 us
    pallas_call x1, Pallas kernels: 237 us -> 216 us  [_block(): pl.pallas_call(functools.partial(_kernel, 4 * dh), name='block', out_shap...]
    unnamed x4 -> x2, local copies, waits for them, and re-layouts: 6.3 us -> 3.68 us
where the time goes in v4:
time: 221 us; the launch traced here: 220 us
  Pallas kernels  216 us (98%)
  local copies, waits for them, and re-layouts  3.68 us (2%)
    pallas_call x1, Pallas kernels, _block(): pl.pallas_call(functools.partial(_kernel, 4 * dh), name='block', out_shap...  216 us

profile of v4, /device:TPU:0, one launch (start us, length us, event | category | flops | bytes accessed | tf_op | source)
XLA Modules:
  0.0 220.4 jit_solution(6631973252818875726)
XLA Ops:
  0.6 216.1 %block.1 = (bf16[32,2,4,16,512]{4,3,2,1,0:T(8,128)(2,1)S(1)}, bf16[32,128,384]{2,1,0:T(8,128)(2,1)S(1)}) custom-call(bf16[4,8,8,16,512]{4,3,2,1,0:T(8,128)(2,1)} %bitcast.8, f32[1,512]{1,0:T(1,128)} %bitcast.10, f32[1,512]{1,0:T(1,128)} %bitcast.11, bf16[512,1024]{1,0:T(8,128)(2,1)} %wg_ref.1, bf16[512,1024]{1,0:T(8,128)(2,1)} %wu_ref.1, ...), custom_call_target="tpu_custom_call" | custom-call | tf_op jit(solution)/shard_map/block/pallas_call | solution.py:481
  216.8 2.0 copy.13
  218.8 1.7 copy.14

commit v5 on v4

--- a/solution.py
+++ b/solution.py
@@ -375,10 +375,10 @@
             out_q_from(u // 4, 2).wait_recv()
             q_fwd(u // 4).start()
 
-    @pl.loop(0, NU + 10)
+    @pl.loop(0, NU + 19)
     def _(t):
-        for lag, fn in ((0, p_compute), (2, p_y), (3, p_h2), (4, p_h3), (5, p_fin), (6, p_g1),
-                        (7, p_g2), (8, p_g3), (9, p_out), (10, p_q)):
+        for lag, fn in ((0, p_compute), (3, p_y), (5, p_h2), (7, p_h3), (9, p_fin), (11, p_g1),
+                        (13, p_g2), (15, p_g3), (17, p_out), (19, p_q)):
             at(t, lag, fn)
 
     for cp in gcopies:

time: 221 us -> 227 us (1.027)
  Pallas kernels: 216 us -> 223 us
    pallas_call x1, Pallas kernels: 216 us -> 223 us  [_block(): pl.pallas_call(functools.partial(_kernel, 4 * dh), name='block', out_shap...]
where the time goes in v5:
time: 227 us
  Pallas kernels  223 us (98%)
  local copies, waits for them, and re-layouts  3.68 us (2%)
    pallas_call x1, Pallas kernels, _block(): pl.pallas_call(functools.partial(_kernel, 4 * dh), name='block', out_shap...  223 us

profile of v5, /device:TPU:0, one launch (start us, length us, event | category | flops | bytes accessed | tf_op | source)
XLA Modules:
  0.0 226.9 jit_solution(10984816801142650851)
XLA Ops:
  0.6 222.5 %block.1 = (bf16[32,2,4,16,512]{4,3,2,1,0:T(8,128)(2,1)S(1)}, bf16[32,128,384]{2,1,0:T(8,128)(2,1)S(1)}) custom-call(bf16[4,8,8,16,512]{4,3,2,1,0:T(8,128)(2,1)} %bitcast.8, f32[1,512]{1,0:T(1,128)} %bitcast.10, f32[1,512]{1,0:T(1,128)} %bitcast.11, bf16[512,1024]{1,0:T(8,128)(2,1)} %wg_ref.1, bf16[512,1024]{1,0:T(8,128)(2,1)} %wu_ref.1, ...), custom_call_target="tpu_custom_call" | custom-call | tf_op jit(solution)/shard_map/block/pallas_call | solution.py:481
  223.2 2.0 copy.13
  225.2 1.7 copy.14

commit v6 on v5

--- a/solution.py
+++ b/solution.py
@@ -13,7 +13,8 @@
 
 NS = 8
 NU = 32
-NE = 6
+NE = 5
+ND = 4
 NJ = 4
 STAGES = 5
 
@@ -24,8 +25,8 @@
 
 def _kernel(d_model, x_ref, g1_ref, g2_ref, wg_ref, wu_ref, wd_ref, o_ref, wo_ref, wq_ref,
             outx_ref, outq_ref,
-            xt, n, g1b, g2b, wg, wu, wd, wo, wq, ot, a, yb, yr, upr, dnr, xg, nq, qb,
-            loc, gs, gr, xs, xr, ws, wr, bs, br, ps, pr, zs, zr, qs, qr):
+            xt, n, g1b, g2b, wg, wu, wd, wo, wq, ot, a, yb, yr, upr, dnr, dbuf, xg, nq, qb,
+            loc, gs, gr, xs, xr, ws, wr, bs, br, ps, pr, zs, zr, ds, dr, qs, qr):
     f, h = lax.axis_index('f'), lax.axis_index('h')
     z, y = f // 2, f % 2
     xx, c = h // 2, h % 2
@@ -208,15 +209,20 @@
     def out_q_local(s):
         return pltpu.make_async_copy(qb.at[s], outq_ref.at[h * NS + s], qs.at[0, s])
 
-    def at(t, lag, fn):
+    def at(t, lag, fn, lo=0, hi=NU):
         i = t - lag
 
-        @pl.when((i >= 0) & (i < NU))
-        def _():
-            late = i // (4 * NE)
-            s = (1 - late) * ((i % (2 * NE)) // 2) + late * (i // 4)
-            k = (1 - late) * (2 * (i // (2 * NE)) + i % 2) + late * ((i + 2) % 4)
-            fn(4 * s + k)
+        @pl.when((i >= lo) & (i < hi))
+        def _():
+            p = i // 2 - NE
+            early = 1 - (p + NE) // NE + (p + NE) // (2 * NE) + (p + NE) // (3 * NE)
+            near_a, near_b = (p % 3) // 2, p // 10
+            s_a = (1 - near_a) * (2 * (p // 3) + p % 3) + near_a * (NE + p // 3)
+            s_b = (1 - near_b) * (p - 2) + near_b * (NS - 1)
+            last = p // 6
+            s = early * (p + NE) + (1 - early) * ((1 - last) * s_a + last * s_b)
+            near = early + (1 - early) * ((1 - last) * near_a + last * near_b)
+            fn(4 * s + 2 * (1 - near) + i % 2)
 
     def p_compute(u):
         s, b = u // 4, hx(u % 4)
@@ -330,7 +336,7 @@
         p_fwd(u, 2)
 
     def done(u):
-        return ((u % 4 == 3) & (u < 4 * NE)) | ((u % 4 == 1) & (u >= 4 * NE))
+        return ((u % 4 == 3) & (u != NU - 1)) | (u == NU - 3)
 
     def p_out(u):
         p_fwd(u, 3)
@@ -339,6 +345,47 @@
         def _():
             b_fwd(2).wait_recv()
 
+        finish(u)
+
+    def d_rs(u, i):
+        e = u - (NU - ND)
+        return remote(yb.at[u, y * 4 + (z + i) % 4], dbuf.at[e, i - 1], ds.at[0, e, i], dr.at[0, e, i],
+                      dev((f + 2 * i) % 8, h))
+
+    def d_ag(u, i):
+        e = u - (NU - ND)
+        v = xg.at[u, y, z]
+        return remote(v, v, ds.at[1, e, i], dr.at[1, e, i], dev((f + 2 * i) % 8, h))
+
+    def d_agy(u):
+        return remote(xg.at[u, y], xg.at[u, y], ps.at[3, u], pr.at[3, u], ypeer)
+
+    def d_y(u):
+        st_y(u).wait_recv()
+        rows = pl.ds(y * 4, 4)
+        yb[u, rows] = yb[u, rows] + yr[u]
+        for i in (2, 1, 3):
+            d_rs(u, i).start()
+
+    def d_fin(u):
+        s, b, e = u // 4, hx(u % 4), u - (NU - ND)
+        for i in range(1, 4):
+            d_rs(u, i).wait_recv()
+        v = (yb[u, y * 4 + z] + dbuf[e, 0]) + (dbuf[e, 1] + dbuf[e, 2])
+        xg[u, y, z] = (xt[b, s, y * 4 + z].astype(F32) + v).astype(BF)
+        for i in (2, 1, 3):
+            d_ag(u, i).start()
+
+    def d_g(u):
+        for i in range(1, 4):
+            d_ag(u, i).wait_recv()
+        d_agy(u).start()
+
+    def d_out(u):
+        d_agy(u).wait_recv()
+        finish(u)
+
+    def finish(u):
         @pl.when(u % 4 == 0)
         def _():
             out_x_local(u).start()
@@ -375,11 +422,14 @@
             out_q_from(u // 4, 2).wait_recv()
             q_fwd(u // 4).start()
 
-    @pl.loop(0, NU + 19)
+    @pl.loop(0, NU + 8)
     def _(t):
-        for lag, fn in ((0, p_compute), (3, p_y), (5, p_h2), (7, p_h3), (9, p_fin), (11, p_g1),
-                        (13, p_g2), (15, p_g3), (17, p_out), (19, p_q)):
-            at(t, lag, fn)
+        at(t, 0, p_compute)
+        for lag, fn in ((2, p_y), (3, p_h2), (4, p_h3), (5, p_fin), (6, p_g1), (7, p_g2), (8, p_g3),
+                        (9, p_out), (10, p_q)):
+            at(t, lag, fn, hi=NU - ND)
+        for lag, fn in ((2, d_y), (4, d_fin), (5, d_g), (6, d_out), (8, p_q)):
+            at(t, lag, fn, lo=NU - ND)
 
     for cp in gcopies:
         cp.wait_send()
@@ -400,9 +450,8 @@
         b_send(i, core, 1).wait_send()
         b_fwd(i).wait_send()
 
-    @pl.loop(0, NU)
+    @pl.loop(0, NU - ND)
     def _(u):
-        st_y(u).wait_send()
         for zz in range(3):
             @pl.when(z == zz)
             def _():
@@ -421,6 +470,17 @@
             @pl.when((z + d <= 3) & (z > 0))
             def _():
                 ag_z(u, z + d, 1).wait_send()
+
+    @pl.loop(NU - ND, NU)
+    def _(u):
+        for i in range(1, 4):
+            d_rs(u, i).wait_send()
+            d_ag(u, i).wait_send()
+        d_agy(u).wait_send()
+
+    @pl.loop(0, NU)
+    def _(u):
+        st_y(u).wait_send()
 
         @pl.when(u % 4 == 0)
         def _():
@@ -466,6 +526,7 @@
         pltpu.VMEM((NU, 4, ch, dh), F32),
         pltpu.VMEM((NU, 3, ch, dh), F32),
         pltpu.VMEM((NU, 3, ch, dh), F32),
+        pltpu.VMEM((ND, 3, ch, dh), F32),
         pltpu.VMEM((NU, 2, 4, ch, dh), BF),
         pltpu.VMEM((4, ur, dh), BF),
         pltpu.VMEM((NS, ur, nqk), BF),
@@ -476,6 +537,7 @@
         dma((3, 3)), dma((3, 3)),
         dma((STAGES, NU)), dma((STAGES, NU)),
         dma((2, NU, 4)), dma((NU, 4)),
+        dma((2, ND, 4)), dma((2, ND, 4)),
         dma((4, NS)), dma((4, NS)),
     ]
     outx, outq = pl.pallas_call(

time: 227 us -> 223 us (0.982)
  Pallas kernels: 223 us -> 218 us
    pallas_call x1, Pallas kernels: 223 us -> 218 us  [_block(): pl.pallas_call(functools.partial(_kernel, 4 * dh), name='block', out_shap...]
where the time goes in v6:
time: 223 us
  Pallas kernels  218 us (98%)
  local copies, waits for them, and re-layouts  3.68 us (2%)
    pallas_call x1, Pallas kernels, _block(): pl.pallas_call(functools.partial(_kernel, 4 * dh), name='block', out_shap...  218 us

profile of v6, /device:TPU:0, one launch (start us, length us, event | category | flops | bytes accessed | tf_op | source)
XLA Modules:
  0.0 222.6 jit_solution(13877504473614835019)
XLA Ops:
  0.6 218.3 %block.1 = (bf16[32,2,4,16,512]{4,3,2,1,0:T(8,128)(2,1)S(1)}, bf16[32,128,384]{2,1,0:T(8,128)(2,1)S(1)}) custom-call(bf16[4,8,8,16,512]{4,3,2,1,0:T(8,128)(2,1)} %bitcast.8, f32[1,512]{1,0:T(1,128)} %bitcast.10, f32[1,512]{1,0:T(1,128)} %bitcast.11, bf16[512,1024]{1,0:T(8,128)(2,1)} %wg_ref.1, bf16[512,1024]{1,0:T(8,128)(2,1)} %wu_ref.1, ...), custom_call_target="tpu_custom_call" | custom-call | tf_op jit(solution)/shard_map/block/pallas_call | solution.py:543
  218.9 2.0 copy.13
  220.9 1.7 copy.14

commit v7 on v6

--- a/solution.py
+++ b/solution.py
@@ -13,7 +13,7 @@
 
 NS = 8
 NU = 32
-NE = 5
+NE = 4
 ND = 4
 NJ = 4
 STAGES = 5
@@ -216,12 +216,10 @@
         def _():
             p = i // 2 - NE
             early = 1 - (p + NE) // NE + (p + NE) // (2 * NE) + (p + NE) // (3 * NE)
-            near_a, near_b = (p % 3) // 2, p // 10
-            s_a = (1 - near_a) * (2 * (p // 3) + p % 3) + near_a * (NE + p // 3)
-            s_b = (1 - near_b) * (p - 2) + near_b * (NS - 1)
-            last = p // 6
-            s = early * (p + NE) + (1 - early) * ((1 - last) * s_a + last * s_b)
-            near = early + (1 - early) * ((1 - last) * near_a + last * near_b)
+            n_mix = (p % 3) // 2
+            s_mix = (1 - n_mix) * (2 * (p // 3) + p % 3) + n_mix * (NE + p // 3)
+            s = early * (p + NE) + (1 - early) * s_mix
+            near = early + (1 - early) * n_mix
             fn(4 * s + 2 * (1 - near) + i % 2)
 
     def p_compute(u):
@@ -422,13 +420,13 @@
             out_q_from(u // 4, 2).wait_recv()
             q_fwd(u // 4).start()
 
-    @pl.loop(0, NU + 8)
+    @pl.loop(0, NU + 10)
     def _(t):
         at(t, 0, p_compute)
-        for lag, fn in ((2, p_y), (3, p_h2), (4, p_h3), (5, p_fin), (6, p_g1), (7, p_g2), (8, p_g3),
-                        (9, p_out), (10, p_q)):
+        for lag, fn in ((2, p_y), (4, p_h2), (6, p_h3), (7, p_fin), (9, p_g1), (10, p_g2), (12, p_g3),
+                        (13, p_out), (14, p_q)):
             at(t, lag, fn, hi=NU - ND)
-        for lag, fn in ((2, d_y), (4, d_fin), (5, d_g), (6, d_out), (8, p_q)):
+        for lag, fn in ((2, d_y), (4, d_fin), (6, d_g), (8, d_out), (10, p_q)):
             at(t, lag, fn, lo=NU - ND)
 
     for cp in gcopies:

time: 223 us -> 224 us (level)
  no operation moved by 1% of the time
where the time goes in v7:
time: 224 us; the launch traced here: 223 us
  Pallas kernels  219 us (98%)
  local copies, waits for them, and re-layouts  3.68 us (2%)
    pallas_call x1, Pallas kernels, _block(): pl.pallas_call(functools.partial(_kernel, 4 * dh), name='block', out_shap...  219 us

profile of v7, /device:TPU:0, one launch (start us, length us, event | category | flops | bytes accessed | tf_op | source)
XLA Modules:
  0.0 223.4 jit_solution(3128726475884011630)
XLA Ops:
  0.6 219.1 %block.1 = (bf16[32,2,4,16,512]{4,3,2,1,0:T(8,128)(2,1)S(1)}, bf16[32,128,384]{2,1,0:T(8,128)(2,1)S(1)}) custom-call(bf16[4,8,8,16,512]{4,3,2,1,0:T(8,128)(2,1)} %bitcast.8, f32[1,512]{1,0:T(1,128)} %bitcast.10, f32[1,512]{1,0:T(1,128)} %bitcast.11, bf16[512,1024]{1,0:T(8,128)(2,1)} %wg_ref.1, bf16[512,1024]{1,0:T(8,128)(2,1)} %wu_ref.1, ...), custom_call_target="tpu_custom_call" | custom-call | tf_op jit(solution)/shard_map/block/pallas_call | solution.py:541
  219.7 2.0 copy.13
  221.7 1.7 copy.14

commit v8 on v7

--- a/solution.py
+++ b/solution.py
@@ -13,7 +13,6 @@
 
 NS = 8
 NU = 32
-NE = 4
 ND = 4
 NJ = 4
 STAGES = 5
@@ -214,13 +213,11 @@
 
         @pl.when((i >= lo) & (i < hi))
         def _():
-            p = i // 2 - NE
-            early = 1 - (p + NE) // NE + (p + NE) // (2 * NE) + (p + NE) // (3 * NE)
-            n_mix = (p % 3) // 2
-            s_mix = (1 - n_mix) * (2 * (p // 3) + p % 3) + n_mix * (NE + p // 3)
-            s = early * (p + NE) + (1 - early) * s_mix
-            near = early + (1 - early) * n_mix
-            fn(4 * s + 2 * (1 - near) + i % 2)
+            p = i // 2
+            q = (2 * p) // NS
+            far = (q + 2) // 3 - q // 3
+            s = p - (NS // 2) * ((q + 2) // 3 + q // 3)
+            fn(4 * s + 2 * far + i % 2)
 
     def p_compute(u):
         s, b = u // 4, hx(u % 4)
@@ -334,7 +331,10 @@
         p_fwd(u, 2)
 
     def done(u):
-        return ((u % 4 == 3) & (u != NU - 1)) | (u == NU - 3)
+        return ((u % 4 == 3) & (u < NU // 2)) | ((u % 4 == 1) & (u >= NU // 2))
+
+    def straight(u):
+        return (u >= NU - 2 * ND) & (u % 4 < 2)
 
     def p_out(u):
         p_fwd(u, 3)
@@ -345,13 +345,16 @@
 
         finish(u)
 
+    def nth(u):
+        return (u - (NU - 2 * ND)) // 4 * 2 + u % 4
+
     def d_rs(u, i):
-        e = u - (NU - ND)
+        e = nth(u)
         return remote(yb.at[u, y * 4 + (z + i) % 4], dbuf.at[e, i - 1], ds.at[0, e, i], dr.at[0, e, i],
                       dev((f + 2 * i) % 8, h))
 
     def d_ag(u, i):
-        e = u - (NU - ND)
+        e = nth(u)
         v = xg.at[u, y, z]
         return remote(v, v, ds.at[1, e, i], dr.at[1, e, i], dev((f + 2 * i) % 8, h))
 
@@ -366,7 +369,7 @@
             d_rs(u, i).start()
 
     def d_fin(u):
-        s, b, e = u // 4, hx(u % 4), u - (NU - ND)
+        s, b, e = u // 4, hx(u % 4), nth(u)
         for i in range(1, 4):
             d_rs(u, i).wait_recv()
         v = (yb[u, y * 4 + z] + dbuf[e, 0]) + (dbuf[e, 1] + dbuf[e, 2])
@@ -448,8 +451,7 @@
         b_send(i, core, 1).wait_send()
         b_fwd(i).wait_send()
 
-    @pl.loop(0, NU - ND)
-    def _(u):
+    def line_sent(u):
         for zz in range(3):
             @pl.when(z == zz)
             def _():
@@ -469,8 +471,7 @@
             def _():
                 ag_z(u, z + d, 1).wait_send()
 
-    @pl.loop(NU - ND, NU)
-    def _(u):
+    def straight_sent(u):
         for i in range(1, 4):
             d_rs(u, i).wait_send()
             d_ag(u, i).wait_send()
@@ -479,6 +480,14 @@
     @pl.loop(0, NU)
     def _(u):
         st_y(u).wait_send()
+
+        @pl.when(straight(u))
+        def _():
+            straight_sent(u)
+
+        @pl.when(jnp.logical_not(straight(u)))
+        def _():
+            line_sent(u)
 
         @pl.when(u % 4 == 0)
         def _():

time: 224 us -> 222 us (level)
  no operation moved by 1% of the time
where the time goes in v8:
time: 222 us
  Pallas kernels  217 us (98%)
  local copies, waits for them, and re-layouts  3.68 us (2%)
    pallas_call x1, Pallas kernels, _block(): pl.pallas_call(functools.partial(_kernel, 4 * dh), name='block', out_shap...  217 us

profile of v8, /device:TPU:0, one launch (start us, length us, event | category | flops | bytes accessed | tf_op | source)
XLA Modules:
  0.0 221.7 jit_solution(11283270705506164888)
XLA Ops:
  0.6 217.4 %block.1 = (bf16[32,2,4,16,512]{4,3,2,1,0:T(8,128)(2,1)S(1)}, bf16[32,128,384]{2,1,0:T(8,128)(2,1)S(1)}) custom-call(bf16[4,8,8,16,512]{4,3,2,1,0:T(8,128)(2,1)} %bitcast.8, f32[1,512]{1,0:T(1,128)} %bitcast.10, f32[1,512]{1,0:T(1,128)} %bitcast.11, bf16[512,1024]{1,0:T(8,128)(2,1)} %wg_ref.1, bf16[512,1024]{1,0:T(8,128)(2,1)} %wu_ref.1, ...), custom_call_target="tpu_custom_call" | custom-call | tf_op jit(solution)/shard_map/block/pallas_call | solution.py:550
  218.0 2.0 copy.13
  220.0 1.7 copy.14

commit v9 on v8

--- a/solution.py
+++ b/solution.py
@@ -423,11 +423,11 @@
             out_q_from(u // 4, 2).wait_recv()
             q_fwd(u // 4).start()
 
-    @pl.loop(0, NU + 10)
+    @pl.loop(0, NU + 18)
     def _(t):
         at(t, 0, p_compute)
         for lag, fn in ((2, p_y), (4, p_h2), (6, p_h3), (7, p_fin), (9, p_g1), (10, p_g2), (12, p_g3),
-                        (13, p_out), (14, p_q)):
+                        (13, p_out), (22, p_q)):
             at(t, lag, fn, hi=NU - ND)
         for lag, fn in ((2, d_y), (4, d_fin), (6, d_g), (8, d_out), (10, p_q)):
             at(t, lag, fn, lo=NU - ND)

time: 222 us -> 213 us (0.959)
  Pallas kernels: 217 us -> 208 us
    pallas_call x1, Pallas kernels: 217 us -> 208 us  [_block(): pl.pallas_call(functools.partial(_kernel, 4 * dh), name='block', out_shap...]
where the time goes in v9:
time: 213 us; the launch traced here: 212 us
  Pallas kernels  208 us (98%)
  local copies, waits for them, and re-layouts  3.68 us (2%)
    pallas_call x1, Pallas kernels, _block(): pl.pallas_call(functools.partial(_kernel, 4 * dh), name='block', out_shap...  208 us

profile of v9, /device:TPU:0, one launch (start us, length us, event | category | flops | bytes accessed | tf_op | source)
XLA Modules:
  0.0 212.4 jit_solution(12116477122537835055)
XLA Ops:
  0.6 208.1 %block.1 = (bf16[32,2,4,16,512]{4,3,2,1,0:T(8,128)(2,1)S(1)}, bf16[32,128,384]{2,1,0:T(8,128)(2,1)S(1)}) custom-call(bf16[4,8,8,16,512]{4,3,2,1,0:T(8,128)(2,1)} %bitcast.8, f32[1,512]{1,0:T(1,128)} %bitcast.10, f32[1,512]{1,0:T(1,128)} %bitcast.11, bf16[512,1024]{1,0:T(8,128)(2,1)} %wg_ref.1, bf16[512,1024]{1,0:T(8,128)(2,1)} %wu_ref.1, ...), custom_call_target="tpu_custom_call" | custom-call | tf_op jit(solution)/shard_map/block/pallas_call | solution.py:550
  208.8 2.0 copy.13
  210.8 1.7 copy.14

commit v10 on v9

--- a/solution.py
+++ b/solution.py
@@ -13,6 +13,7 @@
 
 NS = 8
 NU = 32
+NE = 3
 ND = 4
 NJ = 4
 STAGES = 5
@@ -214,9 +215,9 @@
         @pl.when((i >= lo) & (i < hi))
         def _():
             p = i // 2
-            q = (2 * p) // NS
-            far = (q + 2) // 3 - q // 3
-            s = p - (NS // 2) * ((q + 2) // 3 + q // 3)
+            q = (p + NS - NE) // NS
+            far = q % 2
+            s = p - NE * q - (NS - 2 * NE) * (q // 2)
             fn(4 * s + 2 * far + i % 2)
 
     def p_compute(u):
@@ -331,10 +332,7 @@
         p_fwd(u, 2)
 
     def done(u):
-        return ((u % 4 == 3) & (u < NU // 2)) | ((u % 4 == 1) & (u >= NU // 2))
-
-    def straight(u):
-        return (u >= NU - 2 * ND) & (u % 4 < 2)
+        return ((u % 4 == 3) & (u < 4 * NE)) | ((u % 4 == 1) & (u >= 4 * NE))
 
     def p_out(u):
         p_fwd(u, 3)
@@ -417,41 +415,37 @@
         rows = outq_ref.at[hx(2) * NS + s]
         return remote(rows, rows, qs.at[3, s], qr.at[3, s], core)
 
+    def hand_q(s):
+        out_q_from(s, 2).wait_recv()
+        q_fwd(s).start()
+
     def p_q(u):
         @pl.when(done(u))
         def _():
-            out_q_from(u // 4, 2).wait_recv()
-            q_fwd(u // 4).start()
-
-    @pl.loop(0, NU + 18)
-    def _(t):
-        at(t, 0, p_compute)
-        for lag, fn in ((2, p_y), (4, p_h2), (6, p_h3), (7, p_fin), (9, p_g1), (10, p_g2), (12, p_g3),
-                        (13, p_out), (22, p_q)):
-            at(t, lag, fn, hi=NU - ND)
-        for lag, fn in ((2, d_y), (4, d_fin), (6, d_g), (8, d_out), (10, p_q)):
-            at(t, lag, fn, lo=NU - ND)
-
-    for cp in gcopies:
-        cp.wait_send()
-    x_core.wait_send()
-    x_cross(2).wait_send()
-    x_cross(3).wait_send()
-    for i in range(4):
-        x_y(i).wait_send()
-    for i in range(1, 4):
-        x_z(i).wait_send()
-    for j in range(NJ):
-        for i in range(2):
-            w_send(i, j, across, 0).wait_send()
-            w_send(i, j, core, 1).wait_send()
-            w_fwd(i, j).wait_send()
-    for i in range(3):
-        b_send(i, across, 0).wait_send()
-        b_send(i, core, 1).wait_send()
-        b_fwd(i).wait_send()
+            hand_q(u // 4)
+
+    def prologue_sent():
+        for cp in gcopies:
+            cp.wait_send()
+        x_core.wait_send()
+        x_cross(2).wait_send()
+        x_cross(3).wait_send()
+        for i in range(4):
+            x_y(i).wait_send()
+        for i in range(1, 4):
+            x_z(i).wait_send()
+        for j in range(NJ):
+            for i in range(2):
+                w_send(i, j, across, 0).wait_send()
+                w_send(i, j, core, 1).wait_send()
+                w_fwd(i, j).wait_send()
+        for i in range(3):
+            b_send(i, across, 0).wait_send()
+            b_send(i, core, 1).wait_send()
+            b_fwd(i).wait_send()
 
     def line_sent(u):
+        st_y(u).wait_send()
         for zz in range(3):
             @pl.when(z == zz)
             def _():
@@ -472,23 +466,37 @@
                 ag_z(u, z + d, 1).wait_send()
 
     def straight_sent(u):
+        st_y(u).wait_send()
         for i in range(1, 4):
             d_rs(u, i).wait_send()
             d_ag(u, i).wait_send()
         d_agy(u).wait_send()
 
+    @pl.loop(0, NU + 9)
+    def _(t):
+        at(t, 0, p_compute)
+        for lag, fn in ((2, p_y), (4, p_h2), (6, p_h3), (7, p_fin), (9, p_g1), (10, p_g2), (12, p_g3),
+                        (13, p_out)):
+            at(t, lag, fn, hi=NU - ND)
+        for lag, fn in ((2, d_y), (4, d_fin), (6, d_g), (8, d_out)):
+            at(t, lag, fn, lo=NU - ND)
+        at(t, 20, line_sent)
+        at(t, 22, p_q)
+
+        @pl.when(t == NU - 4)
+        def _():
+            prologue_sent()
+
+    for s in range(NE, NS):
+        hand_q(s)
+
+    @pl.loop(NU + 9, NU + 20)
+    def _(t):
+        at(t, 20, line_sent, hi=NU - ND)
+        at(t, 20, straight_sent, lo=NU - ND)
+
     @pl.loop(0, NU)
     def _(u):
-        st_y(u).wait_send()
-
-        @pl.when(straight(u))
-        def _():
-            straight_sent(u)
-
-        @pl.when(jnp.logical_not(straight(u)))
-        def _():
-            line_sent(u)
-
         @pl.when(u % 4 == 0)
         def _():
             out_x_local(u).wait()

time: 213 us -> 218 us (1.023)
  Pallas kernels: 208 us -> 214 us
    pallas_call x1, Pallas kernels: 208 us -> 214 us  [_block(): pl.pallas_call(functools.partial(_kernel, 4 * dh), name='block', out_shap...]
where the time goes in v10:
time: 218 us
  Pallas kernels  214 us (98%)
  local copies, waits for them, and re-layouts  3.68 us (2%)
    pallas_call x1, Pallas kernels, _block(): pl.pallas_call(functools.partial(_kernel, 4 * dh), name='block', out_shap...  214 us

profile of v10, /device:TPU:0, one launch (start us, length us, event | category | flops | bytes accessed | tf_op | source)
XLA Modules:
  0.0 218.3 jit_solution(2252424882936574463)
XLA Ops:
  0.6 214.0 %block.1 = (bf16[32,2,4,16,512]{4,3,2,1,0:T(8,128)(2,1)S(1)}, bf16[32,128,384]{2,1,0:T(8,128)(2,1)S(1)}) custom-call(bf16[4,8,8,16,512]{4,3,2,1,0:T(8,128)(2,1)} %bitcast.8, f32[1,512]{1,0:T(1,128)} %bitcast.10, f32[1,512]{1,0:T(1,128)} %bitcast.11, bf16[512,1024]{1,0:T(8,128)(2,1)} %wg_ref.1, bf16[512,1024]{1,0:T(8,128)(2,1)} %wu_ref.1, ...), custom_call_target="tpu_custom_call" | custom-call | tf_op jit(solution)/shard_map/block/pallas_call | solution.py:558
  214.6 2.0 copy.13
  216.7 1.7 copy.14

commit v11 on v9

--- a/solution.py
+++ b/solution.py
@@ -426,8 +426,8 @@
     @pl.loop(0, NU + 18)
     def _(t):
         at(t, 0, p_compute)
-        for lag, fn in ((2, p_y), (4, p_h2), (6, p_h3), (7, p_fin), (9, p_g1), (10, p_g2), (12, p_g3),
-                        (13, p_out), (22, p_q)):
+        for lag, fn in ((2, p_y), (4, p_h2), (6, p_h3), (8, p_fin), (10, p_g1), (11, p_g2), (13, p_g3),
+                        (14, p_out), (22, p_q)):
             at(t, lag, fn, hi=NU - ND)
         for lag, fn in ((2, d_y), (4, d_fin), (6, d_g), (8, d_out), (10, p_q)):
             at(t, lag, fn, lo=NU - ND)

time: 213 us -> 216 us (1.014)
  Pallas kernels: 208 us -> 211 us
    pallas_call x1, Pallas kernels: 208 us -> 211 us  [_block(): pl.pallas_call(functools.partial(_kernel, 4 * dh), name='block', out_shap...]
where the time goes in v11:
time: 216 us
  Pallas kernels  211 us (98%)
  local copies, waits for them, and re-layouts  3.68 us (2%)
    pallas_call x1, Pallas kernels, _block(): pl.pallas_call(functools.partial(_kernel, 4 * dh), name='block', out_shap...  211 us

profile of v11, /device:TPU:0, one launch (start us, length us, event | category | flops | bytes accessed | tf_op | source)
XLA Modules:
  0.0 215.5 jit_solution(5008199919452154265)
XLA Ops:
  0.6 211.2 %block.1 = (bf16[32,2,4,16,512]{4,3,2,1,0:T(8,128)(2,1)S(1)}, bf16[32,128,384]{2,1,0:T(8,128)(2,1)S(1)}) custom-call(bf16[4,8,8,16,512]{4,3,2,1,0:T(8,128)(2,1)} %bitcast.8, f32[1,512]{1,0:T(1,128)} %bitcast.10, f32[1,512]{1,0:T(1,128)} %bitcast.11, bf16[512,1024]{1,0:T(8,128)(2,1)} %wg_ref.1, bf16[512,1024]{1,0:T(8,128)(2,1)} %wu_ref.1, ...), custom_call_target="tpu_custom_call" | custom-call | tf_op jit(solution)/shard_map/block/pallas_call | solution.py:550
  211.8 2.0 copy.13
  213.9 1.7 copy.14
